TPU v7x, 32 devices: a whole 2x2x4 slice. The times are simulated.
32 devices in a mesh: stream: 4 (over z), patch: 8 (over y, x, core).
Axes of the slice: x: 2, y: 2, z: 4, core: 2. Of those that a mesh axis runs over, the one named last changes fastest.
Arguments:
- tokens: bfloat16 [4, 1024, 1536], P('stream', 'patch'), may hold values from -6 to 6
- query_weight: bfloat16 [1536, 768], P('stream'), may hold values from -0.25 to 0.25
- key_weight: bfloat16 [1536, 768], P('stream'), may hold values from -0.25 to 0.25
- value_weight: bfloat16 [1536, 768], P('stream'), may hold values from -0.15625 to 0.15625
- cache_keys: bfloat16 [4, 6144, 768], P('stream', 'patch'), may hold values from -240 to 240, as said below
- cache_values: bfloat16 [4, 6144, 768], P('stream', 'patch'), may hold values from -6 to 6
- lengths: int32 [4, 8], P('stream', 'patch'), may hold values from 1 to 6, as said below
- assign: int32 [4, 256, 1], P('stream', 'patch'), may hold values from 0 to 7; in each aligned block of 32 rows (0 to 31, 32 to 63, ..., all dimensions but the last counted through in order) at most 8 rows name the same one
Outputs:
- attended: bfloat16 [4, 1024, 768], P('stream', 'patch')
- new_keys: bfloat16 [4, 2048, 768], P('stream', 'patch')
- new_values: bfloat16 [4, 2048, 768], P('stream', 'patch')
Inputs may be any that keep to these rules, and one draw needn't show every extreme that they name: `lengths`: each stream's owners hold whole cache blocks of 128 tokens; in every stream exactly two owners hold 6 blocks and every other owner 1 or 2. `assign`: among the 32 groups of one device no owner is named more than 8 times. `cache_keys`: rows past an owner's length are not part of its cache.
All inputs are finite; a program needn't handle non-finite values.
Results may differ from a plain program's by a relative error of at most 0.015.
The roundings to bfloat16 on the way count: a program that leaves them out, or rounds other values in their place, can miss the bound.
Values may be sent and summed in bfloat16 or wider, within the bound.
No kernel may reach another device: no remote copies, remote signals or barrier semaphores. Data moves between devices by JAX's collectives and lax.ppermute only.
A program may use at most 128 MiB of HBM per device.

v0:
```python
import math

import jax
import jax.numpy as jnp
from jax import lax
from jax.sharding import PartitionSpec as P

HEADS = 6
HD = 128
BLOCK = 128
APP = 4


epsilon = 1e-06
masked_score = -1e30


def body(tokens, query_weight, key_weight, value_weight, cache_keys, cache_values, lengths, assign):
    owners = lax.axis_size("patch")
    span_rows = tokens.shape[1]
    width = HEADS * HD
    floats = tokens[0].astype(jnp.float32)
    normed = (
        floats * lax.rsqrt(jnp.mean(floats * floats, axis=-1, keepdims=True) + epsilon)
    ).astype(jnp.bfloat16)
    gathered = lax.all_gather(normed, "stream", axis=0, tiled=True)
    shard_rows = query_weight.shape[0]
    offset = lax.axis_index("stream") * shard_rows
    columns = lax.dynamic_slice_in_dim(gathered, offset, shard_rows, 1)
    joined = jnp.concatenate((query_weight, key_weight, value_weight), axis=1)
    joined_sum = lax.psum_scatter(
        jnp.dot(columns, joined, preferred_element_type=jnp.float32),
        "stream",
        scatter_dimension=0,
        tiled=True,
    )
    query_sum = joined_sum[:, :width]
    key_sum = joined_sum[:, width : 2 * width]
    value_sum = joined_sum[:, 2 * width :]
    queries = query_sum.astype(jnp.bfloat16)
    keys_new = key_sum.astype(jnp.bfloat16)
    values_new = value_sum.astype(jnp.bfloat16)
    group_count = span_rows // APP
    most_slots = max(2, 2 * group_count // owners)
    owner_ids = assign[0, :, 0]
    positions = jnp.arange(group_count, dtype=jnp.int32)
    earlier = positions[None, :] < positions[:, None]
    matches = owner_ids[:, None] == owner_ids[None, :]
    ranks = jnp.sum(jnp.logical_and(matches, earlier).astype(jnp.int32), axis=1)
    targets = owner_ids * most_slots + ranks
    slot_ids = jnp.arange(owners * most_slots, dtype=jnp.int32)
    select = (targets[None, :] == slot_ids[:, None]).astype(jnp.bfloat16)
    grouped = jnp.concatenate(
        (keys_new.reshape(group_count, APP * width), values_new.reshape(group_count, APP * width)),
        axis=1,
    )
    outgoing = jnp.dot(select, grouped, preferred_element_type=jnp.float32).astype(jnp.bfloat16)
    flags_out = jnp.sum(select.astype(jnp.float32), axis=1).astype(jnp.bfloat16)
    incoming, flags_in = (
        lax.all_to_all(outgoing, "patch", split_axis=0, concat_axis=0, tiled=True),
        lax.all_to_all(flags_out, "patch", split_axis=0, concat_axis=0, tiled=True),
    )
    slot_rows = incoming.shape[0] * APP
    app_keys = incoming[:, : APP * width].reshape(slot_rows, width)
    app_values = incoming[:, APP * width :].reshape(slot_rows, width)
    row_valid = jnp.repeat(flags_in, APP) > 0.5
    all_queries = lax.all_gather(queries, "patch", axis=0, tiled=True).reshape(-1, HEADS, HD)
    scale = 1.0 / math.sqrt(HD)
    cache_k = cache_keys[0]
    cache_v = cache_values[0]
    block_count = lengths[0, 0]

    def fold_block(state, key_rows, value_rows, live):
        best, numer_acc, total_acc = state
        scores = (
            jnp.einsum(
                "thd,khd->thk",
                all_queries,
                key_rows.reshape(-1, HEADS, HD),
                preferred_element_type=jnp.float32,
            )
            * scale
        )
        if live is not None:
            scores = jnp.where(live[None, None, :], scores, masked_score)
        block_top = jnp.max(scores, axis=2)
        weights = jnp.exp(scores - block_top[:, :, None])
        if live is not None:
            weights = jnp.where(live[None, None, :], weights, 0.0)
        weights = weights.astype(jnp.bfloat16)
        part_numer = jnp.einsum(
            "thk,khd->thd",
            weights,
            value_rows.reshape(-1, HEADS, HD),
            preferred_element_type=jnp.float32,
        )
        part_total = jnp.sum(weights.astype(jnp.float32), axis=2)
        merged = jnp.maximum(best, block_top)
        old_scale = jnp.exp(best - merged)
        new_scale = jnp.exp(block_top - merged)
        numer_acc = numer_acc * old_scale[:, :, None] + part_numer * new_scale[:, :, None]
        total_acc = total_acc * old_scale + part_total * new_scale
        return (merged, numer_acc, total_acc)

    query_count = all_queries.shape[0]
    start_state = (
        jnp.full((query_count, HEADS), masked_score, jnp.float32),
        jnp.zeros((query_count, HEADS, HD), jnp.float32),
        jnp.zeros((query_count, HEADS), jnp.float32),
    )
    state = fold_block(start_state, app_keys, app_values, row_valid)

    def per_block(block, state):
        key_rows = lax.dynamic_slice_in_dim(cache_k, block * BLOCK, BLOCK, 0)
        value_rows = lax.dynamic_slice_in_dim(cache_v, block * BLOCK, BLOCK, 0)
        return fold_block(state, key_rows, value_rows, None)

    top_row, numer, total = lax.fori_loop(0, block_count, per_block, state)
    got_numer, got_top, got_total = (
        lax.all_to_all(
            numer.reshape(1, -1, width), "patch", split_axis=1, concat_axis=0, tiled=True
        ),
        lax.all_to_all(top_row[None], "patch", split_axis=1, concat_axis=0, tiled=True),
        lax.all_to_all(total[None], "patch", split_axis=1, concat_axis=0, tiled=True),
    )
    best = jnp.max(got_top, axis=0)
    factor = jnp.exp(got_top - best[None])
    sum_numer = jnp.sum(
        got_numer.reshape(owners, span_rows, HEADS, HD) * factor[:, :, :, None], axis=0
    )
    sum_total = jnp.sum(got_total * factor, axis=0)
    result = sum_numer / sum_total[:, :, None]
    attended = result.reshape(1, span_rows, width).astype(jnp.bfloat16)
    return (attended, app_keys[None], app_values[None])


def solution(mesh):
    placed = (
        P("stream", "patch", None),
        P("stream", None),
        P("stream", None),
        P("stream", None),
        P("stream", "patch", None),
        P("stream", "patch", None),
        P("stream", "patch"),
        P("stream", "patch", None),
    )
    return jax.shard_map(
        body,
        mesh=mesh,
        in_specs=placed,
        out_specs=(
            P("stream", "patch", None),
            P("stream", "patch", None),
            P("stream", "patch", None),
        ),
        check_vma=False,
    )
```

profile of v0, /device:TPU:0, one launch (start us, length us, event | category | flops | bytes accessed | tf_op | source)
XLA Modules:
  0.0 303.4 jit_solution(281291631412131650)
XLA Ops:
  7.2 1.2 fusion.16
  8.4 1.9 fusion.17
  10.3 39.8 %all-gather.3.cloned.1.call-done = bf16[512,1536]{1,0:T(8,128)(2,1)} async-done(((bf16[128,1536]{1,0:T(8,128)(2,1)}), bf16[512,1536]{1,0:T(8,128)(2,1)}) %all-gather.3.cloned.1.call-update) | async-done | bytes 1572880 | tf_op jit(solution)/shard_map/all_gather | solution.py:26
  50.2 5.1 %fusion.10 = f32[512,2304]{1,0:T(8,128)} fusion(bf16[384,768]{1,0:T(8,128)(2,1)} %param.13, bf16[384,768]{1,0:T(8,128)(2,1)} %param.12, bf16[384,768]{1,0:T(8,128)(2,1)} %param.11, bf16[512,1536]{1,0:T(8,128)(2,1)} %all-gather.3.cloned.1.call-done, s32[]{:T(128)S(6)} %select_n.17), kind=kOutput, calls=%fused_computation.25 | convolution fusion | flops 911278080 | bytes 6881284 | tf_op jit(solution)/shard_map/dot_general | solution.py:32
  55.3 84.3 %reduce-scatter.2.cloned.1.call-done = f32[128,2304]{1,0:T(8,128)} async-done(((f32[512,2304]{1,0:T(8,128)}), f32[128,2304]{1,0:T(8,128)}) %reduce-scatter.2.cloned.1.call-update) | async-done | bytes 1179664 | tf_op jit(solution)/shard_map/reduce_scatter | solution.py:31
  139.6 1.3 convert.7
  140.9 0.7 fusion.35
  142.6 3.7 %all-to-all-start = ((bf16[8,8,1]{1,2,0:T(2,128)(2,1)}), bf16[8,8,1]{1,2,0:T(2,128)(2,1)S(1)}, u32[]{:S(2)}, u32[]{:S(2)}) async-start(bf16[8,8,1]{1,2,0:T(2,128)(2,1)} %all_to_all.52), calls=%async_computation | async-start | bytes 8192 | tf_op jit(solution)/shard_map/all_to_all | solution.py:61
  146.6 1.4 fusion.5
  147.9 3.0 all-to-all-done
  150.9 3.5 %all-to-all-start.1 = ((bf16[8,8,6144]{2,1,0:T(8,128)(2,1)}), bf16[8,8,6144]{2,1,0:T(8,128)(2,1)S(1)}, u32[]{:S(2)}, u32[]{:S(2)}) async-start(bf16[8,8,6144]{2,1,0:T(8,128)(2,1)} %fusion.5), calls=%async_computation.2 | async-start | bytes 1572864 | tf_op jit(solution)/shard_map/all_to_all | solution.py:60
  154.5 1.5 copy.109
  155.9 1.4 copy.110
  157.7 13.4 %all-to-all-done.1 = bf16[8,8,6144]{2,1,0:T(8,128)(2,1)S(1)} async-done(((bf16[8,8,6144]{2,1,0:T(8,128)(2,1)}), bf16[8,8,6144]{2,1,0:T(8,128)(2,1)S(1)}, u32[]{:S(2)}, u32[]{:S(2)}) %all-to-all-start.1) | async-done | bytes 786464 | tf_op jit(solution)/shard_map/all_to_all | solution.py:60
  171.7 1.3 reshape_reshape.7
  173.0 1.7 copy.104
  174.7 1.6 copy.111
  176.3 1.2 bitcast_reduce_fusion.1
  177.5 2.1 convert_reduce_fusion.1
  180.2 0.9 fusion.9
  181.1 40.9 %while.14 = (s32[]{:T(128)}, f32[1024,6]{0,1:T(8,128)}, f32[1024,6,128]{0,2,1:T(8,128)S(1)}, f32[1024,6]{0,1:T(8,128)}, s32[]{:T(128)}, /*index=5*/bf16[768,768]...) while((s32[]{:T(128)}, f32[1024,6]{0,1:T(8,128)}, ...), condition=%wide.region_9.10_spmd, body=%wide.region_6.9_spmd.sunk | while | flops 412901376 | bytes 19218712 | solution.py:118
  181.7 1.1 constant_dynamic-slice_fusion.3
  182.8 2.1 bitcast_reduce_fusion.3
  186.1 1.6 fusion.50
  188.4 1.1 constant_dynamic-slice_fusion.3
  189.5 2.1 bitcast_reduce_fusion.3
  192.8 1.6 fusion.50
  195.1 1.1 constant_dynamic-slice_fusion.3
  196.2 2.1 bitcast_reduce_fusion.3
  199.5 1.6 fusion.50
  201.8 1.1 constant_dynamic-slice_fusion.3
  202.9 2.1 bitcast_reduce_fusion.3
  206.2 1.6 fusion.50
  208.4 1.1 constant_dynamic-slice_fusion.3
  209.5 2.1 bitcast_reduce_fusion.3
  212.9 1.6 fusion.50
  215.1 1.1 constant_dynamic-slice_fusion.3
  216.2 2.1 bitcast_reduce_fusion.3
  219.5 1.6 fusion.50
  222.0 1.8 copy.113
  224.3 3.8 %reduce.6 = f32[1024,6]{1,0:T(8,128)} reduce(f32[1024,1,6]{2,1,0:T(1,128)} %bitcast.94, f32[]{:T(128)} %broadcast.73), dimensions={1}, to_apply=%bitcast.56.reduce_sub_computation | reduce | bytes 49156
  228.1 2.0 reshape.145
  230.1 3.9 %all-to-all-start.3 = ((f32[8,1,768]{2,1,0:T(1,128)}), f32[8,1,768]{2,1,0:T(1,128)}, u32[]{:S(2)}, u32[]{:S(2)}) async-start(f32[8,1,768]{2,1,0:T(1,128)} %reshape.145), calls=%async_computation.4 | async-start | bytes 49152 | tf_op jit(solution)/shard_map/all_to_all | solution.py:123
  234.1 1.8 copy.117
  235.8 3.8 %reduce.4 = f32[1024,6]{1,0:T(8,128)} reduce(f32[1024,1,6]{2,1,0:T(1,128)} %bitcast.95, f32[]{:T(128)} %broadcast.73), dimensions={1}, to_apply=%bitcast.54.reduce_sub_computation | reduce | bytes 49156
  239.6 2.0 reshape.143
  241.7 4.1 %all-to-all-start.4 = ((f32[8,1,768]{2,1,0:T(1,128)}), f32[8,1,768]{2,1,0:T(1,128)}, u32[]{:S(2)}, u32[]{:S(2)}) async-start(f32[8,1,768]{2,1,0:T(1,128)} %reshape.143), calls=%async_computation.5 | async-start | bytes 49152 | tf_op jit(solution)/shard_map/all_to_all | solution.py:124
  245.8 5.5 %copy.112 = f32[1,1024,768]{2,0,1:T(1,128)} copy(f32[1,1024,768]{1,2,0:T(8,128)S(1)} %bitcast.82) | data formatting | bytes 6291456 | tf_op jit(solution)/shard_map/reshape | solution.py:121
  251.2 4.2 %all-to-all-start.2 = ((f32[1,1024,768]{2,0,1:T(1,128)}), f32[1,1024,768]{2,0,1:T(1,128)S(1)}, u32[]{:S(2)}, u32[]{:S(2)}) async-start(f32[1,1024,768]{2,0,1:T(1,128)} %copy.112), calls=%async_computation.3 | async-start | bytes 6291456 | tf_op jit(solution)/shard_map/all_to_all | solution.py:120
  255.4 2.0 broadcast_in_dim_reshape.6
  257.4 1.0 broadcast_in_dim_reshape.7
  258.4 1.4 reduce.7
  259.8 1.7 reshape.146
  261.5 1.2 copy.124
  262.7 1.1 reduce_max.28
  263.9 1.5 reduce.5
  265.3 1.7 reshape.144
  267.0 1.2 copy.125
  268.3 1.9 mul.117
  270.2 3.6 %copy.116 = f32[1,8,128,768]{3,2,1,0:T(8,128)} copy(f32[1,8,128,768]{2,3,1,0:T(8,128)} %bitcast.88) | data formatting | bytes 6291456 | tf_op jit(solution)/shard_map/mul | solution.py:129
  273.8 0.9 copy.119
  274.8 18.5 %all-to-all-done.2 = f32[1,1024,768]{2,0,1:T(1,128)S(1)} async-done(((f32[1,1024,768]{2,0,1:T(1,128)}), f32[1,1024,768]{2,0,1:T(1,128)S(1)}, u32[]{:S(2)}, u32[]{:S(2)}) %all-to-all-start.2) | async-done | bytes 3145760 | tf_op jit(solution)/shard_map/all_to_all | solution.py:120
  293.5 1.7 copy-done
  296.2 0.7 fusion.21
  (103 shorter events, 12.1 us)
Async XLA Ops:
  7.2 43.0 %all-gather.3.cloned.1.call-start = ((), (), s32[]{:S(2)}) async-start(), calls=%async_computation.6 | async-start | bytes 1966080 | tf_op jit(solution)/shard_map/all_gather | solution.py:26
  10.3 129.3 %reduce-scatter.2.cloned.1.call-start = ((), (), s32[]{:S(2)}) async-start(), calls=%async_computation.7 | async-start | bytes 5898240 | tf_op jit(solution)/shard_map/reduce_scatter | solution.py:31
  55.2 86.4 %copy-start.10 = (s32[1,32,1]{1,2,0:T(1,128)S(1)}, s32[1,32,1]{1,2,0:T(1,128)}, u32[]{:S(2)}) copy-start(s32[1,32,1]{1,2,0:T(1,128)} %param.17) | copy-start | bytes 388
  55.3 99.2 %copy-start.8 = (bf16[1,768,768]{2,1,0:T(8,128)(2,1)S(1)}, bf16[1,768,768]{2,1,0:T(8,128)(2,1)}, u32[]{:S(2)}) copy-start(bf16[1,768,768]{2,1,0:T(8,128)(2,1)} %param.14) | copy-start | bytes 3538948
  55.3 117.7 %all-gather.5.cloned.1.call-start = ((), (), s32[]{:S(2)}) async-start(), calls=%async_computation.8 | async-start | bytes 1769472 | tf_op jit(solution)/shard_map/all_gather | solution.py:67
  141.6 14.3 %copy-start.9 = (bf16[1,768,768]{2,1,0:T(8,128)(2,1)S(1)}, bf16[1,768,768]{2,1,0:T(8,128)(2,1)}, u32[]{:S(2)}) copy-start(bf16[1,768,768]{2,1,0:T(8,128)(2,1)} %param.15) | copy-start | bytes 3538948
  142.6 8.3 %all-to-all-start = ((bf16[8,8,1]{1,2,0:T(2,128)(2,1)}), bf16[8,8,1]{1,2,0:T(2,128)(2,1)S(1)}, u32[]{:S(2)}, u32[]{:S(2)}) async-start(bf16[8,8,1]{1,2,0:T(2,128)(2,1)} %all_to_all.52), calls=%async_computation | async-start | bytes 8192 | tf_op jit(solution)/shard_map/all_to_all | solution.py:61
  150.9 20.2 %all-to-all-start.1 = ((bf16[8,8,6144]{2,1,0:T(8,128)(2,1)}), bf16[8,8,6144]{2,1,0:T(8,128)(2,1)S(1)}, u32[]{:S(2)}, u32[]{:S(2)}) async-start(bf16[8,8,6144]{2,1,0:T(8,128)(2,1)} %fusion.5), calls=%async_computation.2 | async-start | bytes 1572864 | tf_op jit(solution)/shard_map/all_to_all | solution.py:60
  171.2 1.8 copy-start.1
  177.5 2.7 copy-start.2
  182.8 2.7 copy-start.3
  182.8 2.7 copy-start.5
  185.5 0.6 copy-start.4
  185.5 0.6 copy-start.6
  189.5 2.7 copy-start.3
  189.5 2.7 copy-start.5
  192.2 0.6 copy-start.4
  192.2 0.6 copy-start.6
  196.2 2.7 copy-start.3
  196.2 2.7 copy-start.5
  198.9 0.6 copy-start.4
  198.9 0.6 copy-start.6
  202.8 2.7 copy-start.3
  202.8 2.7 copy-start.5
  205.5 0.6 copy-start.4
  205.6 0.6 copy-start.6
  209.5 2.7 copy-start.3
  209.5 2.7 copy-start.5
  212.2 0.6 copy-start.4
  212.2 0.6 copy-start.6
  216.2 2.7 copy-start.3
  216.2 2.7 copy-start.5
  218.9 0.6 copy-start.4
  218.9 0.6 copy-start.6
  230.1 11.5 %all-to-all-start.3 = ((f32[8,1,768]{2,1,0:T(1,128)}), f32[8,1,768]{2,1,0:T(1,128)}, u32[]{:S(2)}, u32[]{:S(2)}) async-start(f32[8,1,768]{2,1,0:T(1,128)} %reshape.145), calls=%async_computation.4 | async-start | bytes 49152 | tf_op jit(solution)/shard_map/all_to_all | solution.py:123
  241.7 9.6 %all-to-all-start.4 = ((f32[8,1,768]{2,1,0:T(1,128)}), f32[8,1,768]{2,1,0:T(1,128)}, u32[]{:S(2)}, u32[]{:S(2)}) async-start(f32[8,1,768]{2,1,0:T(1,128)} %reshape.143), calls=%async_computation.5 | async-start | bytes 49152 | tf_op jit(solution)/shard_map/all_to_all | solution.py:124
  251.2 42.0 %all-to-all-start.2 = ((f32[1,1024,768]{2,0,1:T(1,128)}), f32[1,1024,768]{2,0,1:T(1,128)S(1)}, u32[]{:S(2)}, u32[]{:S(2)}) async-start(f32[1,1024,768]{2,0,1:T(1,128)} %copy.112), calls=%async_computation.3 | async-start | bytes 6291456 | tf_op jit(solution)/shard_map/all_to_all | solution.py:120
  293.3 1.9 copy-start
  295.2 1.0 copy-start.7
Sparse Core Ops, SparseCore 0:
  10.4 39.7 all-gather.2
  55.4 84.1 reduce-scatter.1
  142.0 29.6 all-gather.4
where the time goes:
time: 305 us; the launch traced here: 303 us
  waiting for transfers between devices  159 us (52%)
  local copies, waits for them, and re-layouts  51.4 us (17%)
  matrix products  30.4 us (10%)
  other arithmetic  23.7 us (8%)
  starting transfers between devices  19.5 us (6%)
  between operations  13.9 us (5%)
  loops' own time  5.28 us (2%)
    reduce_scatter x1, waiting for transfers between devices, body(): lax.psum_scatter(jnp.dot(columns, joined, preferred_element_type=jnp.floa...  84.3 us
    all_gather x1, waiting for transfers between devices, body(): gathered = lax.all_gather(normed, 'stream', axis=0, tiled=True)  39.8 us
    all_to_all x1, waiting for transfers between devices, body(): lax.all_to_all(numer.reshape(1, -1, width), 'patch', split_axis=1, concat...  18.5 us
    dot_general x7, matrix products, fold_block(): jnp.einsum('thd,khd->thk', all_queries, key_rows.reshape(-1, HEADS, HD),...  13.5 us
    all_to_all x1, waiting for transfers between devices, body(): lax.all_to_all(outgoing, 'patch', split_axis=0, concat_axis=0, tiled=True)  13.4 us
    unnamed x23, local copies, waits for them, and re-layouts  13.4 us
    dot_general x7, matrix products, fold_block(): jnp.einsum('thk,khd->thd', weights, value_rows.reshape(-1, HEADS, HD), pr...  10.5 us
    unnamed x2, other arithmetic  7.58 us
  transfers between devices with their start and end apart: 8, of which 5 were waited for; matrix products, arithmetic and copies ran while one was open for 13% of the time, Pallas kernels for 0%

commit v1 on v0

v1 whole, which is shorter than its diff:
```python
import functools
import math

import jax
import jax.numpy as jnp
from jax import lax
from jax.experimental import pallas as pl
from jax.experimental.pallas import tpu as pltpu
from jax.sharding import PartitionSpec as P


HEADS = 6
HD = 128
BLOCK = 128
APP = 4
EPS = 1e-06
MASKED = -1e30
WIDTH = HEADS * HD
EXP_SCALE = math.log2(math.e) / math.sqrt(HD)
STAT_ROWS = 32


VMEM = pl.BlockSpec(memory_space=pltpu.VMEM)
SMEM = pl.BlockSpec(memory_space=pltpu.SMEM)
ANY = pl.BlockSpec(memory_space=pl.ANY)
NT = (((1,), (1,)), ((), ()))
TN = (((0,), (0,)), ((), ()))


def call(kernel, out_shape, args, smem=0, hbm=0, scratch=(), sems=(), flops=0, limit=None):
    held = [*args[smem : len(args) - hbm], *jax.tree.leaves(out_shape), *scratch]
    size = sum(math.prod(x.shape) * jnp.dtype(x.dtype).itemsize for x in held)
    limit = limit or min(60 << 20, size * 5 // 4 + (10 << 20))
    return pl.pallas_call(
        kernel,
        out_shape=out_shape,
        in_specs=[SMEM] * smem + [VMEM] * (len(args) - smem - hbm) + [ANY] * hbm,
        out_specs=jax.tree.map(lambda _: VMEM, out_shape),
        scratch_shapes=[*scratch, *sems],
        compiler_params=pltpu.CompilerParams(vmem_limit_bytes=limit),
        cost_estimate=pl.CostEstimate(flops=flops, bytes_accessed=1 << 20, transcendentals=0),
    )(*args)


def peer(axis, r):
    return jnp.bitwise_xor(lax.axis_index(axis).astype(jnp.int32), r)


def chip(s):
    return jnp.right_shift(peer("patch", 2 * s), 1)


def core(j):
    return jnp.bitwise_and(peer("patch", j), 1)


def part(index, size):
    return pl.ds(pl.multiple_of(index * size, size), size)


def normalize_kernel(x_ref, x_out):
    floats = x_ref[...].astype(jnp.float32)
    mean = jnp.mean(floats * floats, axis=1, keepdims=True)
    x_out[...] = (floats * lax.rsqrt(mean + EPS)).astype(jnp.bfloat16)


def columns_kernel(wq_ref, wk_ref, wv_ref, wq_out, wkv_out, w_scr, sems):
    share = wq_out.shape[0]
    window = w_scr.shape[2]
    first = peer("patch", 0) * share
    lanes = jnp.minimum(first - jnp.bitwise_and(first, 127), WIDTH - window)
    copies = []
    for i, w_ref in enumerate((wq_ref, wk_ref, wv_ref)):
        source = w_ref.at[:, pl.ds(pl.multiple_of(lanes, 128), window)]
        copies.append(pltpu.make_async_copy(source, w_scr.at[i], sems.at[i]))
        copies[-1].start()
    row = lax.broadcasted_iota(jnp.int32, (share, window), 0)
    col = lax.broadcasted_iota(jnp.int32, (share, window), 1)
    pick = (col == row + (first - lanes)).astype(jnp.float32).astype(jnp.bfloat16)
    got = []
    for i in range(3):
        copies[i].wait()
        got.append(lax.dot_general(pick, w_scr[i], NT, preferred_element_type=jnp.float32))
    wq_out[...] = got[0].astype(jnp.bfloat16)
    wkv_out[...] = jnp.concatenate(got[1:], axis=0).astype(jnp.bfloat16)


def target_kernel(owners, most, assign_ref, tgt_ref):
    groups = assign_ref.shape[1]
    owner = assign_ref[...]
    ids = lax.broadcasted_iota(jnp.int32, (max(owners, 8), groups), 0)
    named = (ids == owner).astype(jnp.float32)
    r = lax.broadcasted_iota(jnp.int32, (groups, groups), 0)
    c = lax.broadcasted_iota(jnp.int32, (groups, groups), 1)
    before = (r < c).astype(jnp.float32)
    seen = jnp.dot(named, before, preferred_element_type=jnp.float32)
    rank = jnp.sum(seen * named, axis=0, keepdims=True)
    token = lax.broadcasted_iota(jnp.int32, (groups, groups * APP), 1)
    group = lax.broadcasted_iota(jnp.int32, (groups, groups * APP), 0)
    mine = jnp.logical_and(token >= group * APP, token < group * APP + APP).astype(jnp.float32)
    both = jnp.concatenate(
        (
            jnp.broadcast_to(owner.astype(jnp.float32), (8, groups)),
            jnp.broadcast_to(rank, (8, groups)),
        ),
        axis=0,
    )
    both = jnp.dot(both, mine, preferred_element_type=jnp.float32).astype(jnp.int32)
    inner = jnp.bitwise_and(lax.broadcasted_iota(jnp.int32, tgt_ref.shape, 1), APP - 1)
    source = both[0:8] * (owners // 2) + chip(0)
    tgt_ref[...] = source * (most * APP) + both[8:16] * APP + inner


def stage_kernel(k0_ref, v0_ref, k1_ref, v1_ref, kk_ref, vt_ref, v_scr, sems):
    copies = [
        pltpu.make_async_copy(v0_ref, v_scr.at[0], sems.at[0]),
        pltpu.make_async_copy(v1_ref, v_scr.at[1], sems.at[1]),
        pltpu.make_async_copy(k0_ref, kk_ref.at[0], sems.at[2]),
        pltpu.make_async_copy(k1_ref, kk_ref.at[1], sems.at[3]),
    ]
    for copy in copies:
        copy.start()
    for j in range(2):
        copies[j].wait()
        for h in range(HEADS):
            lo, hi = h * HD, (h + 1) * HD
            vt_ref[j, lo:hi, :] = v_scr[j, :, lo:hi].astype(jnp.float32).T.astype(jnp.bfloat16)
    copies[2].wait()
    copies[3].wait()


def gather_weights_kernel(shards, kinds, *refs):
    w_refs, (out_ref, scr) = refs[: 2 * shards], refs[2 * shards :]
    share, depth = w_refs[0].shape[0] // kinds, w_refs[0].shape[1]
    for j in range(2):
        for s in range(shards):
            for i in range(kinds):
                rows = part(core(j) + 2 * i, share)
                piece = w_refs[j * shards + s][...].astype(jnp.float32)
                scr[rows, part(peer("stream", s), depth)] = piece[i * share : (i + 1) * share]
    out_ref[...] = scr[...].astype(jnp.bfloat16)


def project_q_kernel(chips, *refs):
    x_refs, (w_ref, q_ref, x_ref) = refs[:chips], refs[chips:]
    rows = x_refs[0].shape[0]
    for s in range(chips):
        x_ref[part(chip(s), rows), :] = x_refs[s][...]
    q_ref[...] = lax.dot_general(
        w_ref[...], x_ref[...], NT, preferred_element_type=jnp.float32
    ).astype(jnp.bfloat16)


def project_kv_kernel(chips, x_ref, w_ref, kv_ref, *out_refs):
    kv_ref[...] = lax.dot_general(
        w_ref[...], x_ref[...], NT, preferred_element_type=jnp.float32
    ).astype(jnp.bfloat16)
    wide = kv_ref.shape[0] // 2
    rows = x_ref.shape[0] // chips
    for s in range(chips):
        out_refs[s][0] = kv_ref[0:wide, part(chip(s), rows)]
        out_refs[s][1] = kv_ref[wide:, part(chip(s), rows)]


def hits_kernel(chips, *refs):
    t_refs, refs = refs[:chips], refs[chips:]
    out_refs, (t_scr,) = refs[:chips], refs[chips:]
    rows = t_refs[0].shape[1]
    for s in range(chips):
        t_scr[:, part(chip(s), rows)] = t_refs[s][...]
    targets = t_scr[0:1, :]
    slots = out_refs[0].shape[0]
    slot = lax.broadcasted_iota(jnp.int32, (slots, chips * rows), 0)
    for s in range(chips):
        hit = slot == targets - chip(s) * slots
        out_refs[s][...] = hit.astype(jnp.float32).astype(jnp.bfloat16)


def select_kernel(chips, *refs):
    hit_refs, (kv_ref, *out_refs) = refs[:chips], refs[chips:]
    wide = kv_ref.shape[0] // 2
    for s in range(chips):
        got = lax.dot_general(
            kv_ref[...], hit_refs[s][...], NT, preferred_element_type=jnp.float32
        )
        out_refs[s][0] = got[:wide].astype(jnp.bfloat16)
        out_refs[s][1] = got[wide:].astype(jnp.bfloat16)


def each_tile(count, tile, one):
    if count <= 2:
        for j in range(count):
            one(j * tile)
    else:
        lax.fori_loop(
            0, count, lambda j, c: (one(pl.multiple_of(j * tile, tile)), c)[1], 0
        )


def head_group(chips, flip):
    top = jnp.bitwise_and(chip(0), chips // 2) > 0
    return jnp.where(top, 1 - flip, flip) * (HEADS // 2)


def with_ones(value):
    return jnp.concatenate((value, jnp.ones((16, value.shape[1]), value.dtype)), axis=0)


def cached_kernel(chips, flip, tile, len0_ref, len1_ref, *refs):
    q_refs, refs = refs[: chips // 2], refs[chips // 2 :]
    kk_ref, vt_ref, q_all, acc_ref, top_ref, total_ref = refs
    wide = q_refs[0].shape[0]
    for i in range(chips // 2):
        at = jnp.bitwise_and(chip(i), chips // 2 - 1)
        q_all[part(at, wide), :] = q_refs[i][...]
    tokens = q_all.shape[1]
    capacity = kk_ref.shape[1]
    short = min(2 * BLOCK, capacity)
    first = head_group(chips, flip)
    lengths = (len0_ref[0], len1_ref[0])

    def run(sizes):
        def head(h, carry):
            at = part(h, HD)
            row = part(h, 8)
            keys = [kk_ref[i, 0 : sizes[i], part(first + h, HD)] for i in range(2)]
            values = [with_ones(vt_ref[i, part(first + h, HD), 0 : sizes[i]]) for i in range(2)]

            def several(j):
                lanes = [pl.ds(j + t * tile, tile) for t in range(min(2, tokens // tile))]
                scores = []
                for lane in lanes:
                    q = q_all[at, lane]
                    both = []
                    for i in range(2):
                        s = jnp.dot(keys[i], q, preferred_element_type=jnp.float32)
                        if sizes[i] == short:
                            pos = lax.broadcasted_iota(jnp.int32, s.shape, 0)
                            s = jnp.where(pos < lengths[i] * BLOCK, s, MASKED)
                        both.append(s)
                    scores.append(both)
                tops = [
                    jnp.maximum(*[jnp.max(s, axis=0, keepdims=True) for s in both])
                    for both in scores
                ]
                weights = [
                    [jnp.exp2((s - top) * EXP_SCALE).astype(jnp.bfloat16) for s in both]
                    for both, top in zip(scores, tops)
                ]
                numers = [
                    sum(
                        jnp.dot(v, w, preferred_element_type=jnp.float32)
                        for v, w in zip(values, both)
                    )
                    for both in weights
                ]
                for lane, top, numer in zip(lanes, tops, numers):
                    acc_ref[at, lane] = numer[:HD]
                    top_ref[row, lane] = jnp.broadcast_to(top, (8, tile))
                    total_ref[row, lane] = numer[HD : HD + 8]

            step = min(2 * tile, tokens)
            each_tile(tokens // step, step, several)
            return carry

        lax.fori_loop(0, HEADS // 2, head, 0)

    brief = [length * BLOCK <= short for length in lengths]
    if capacity <= short:
        run((short, short))
    else:
        for sizes in ((short, short), (short, capacity), (capacity, short), (capacity, capacity)):
            want = [size == short for size in sizes]
            fits = [b if w else jnp.logical_not(b) for b, w in zip(brief, want)]

            @pl.when(jnp.logical_and(*fits))
            def _(sizes=sizes):
                run(sizes)


def rows_to_levels(stat):
    stat = stat.astype(jnp.float32)
    return stat[0:8] + stat[8:16] + stat[16:24]


def appended_kernel(chips, tile, *refs):
    kv_refs, refs = refs[: 2 * chips], refs[2 * chips :]
    states, refs = (refs[0:4], refs[4:8]), refs[8:]
    out_refs, (kt_scr, vt_scr, out_scr, level_scr) = refs[:chips], refs[chips:]
    wide, rows = kv_refs[0].shape[1], kv_refs[0].shape[2]
    for j in range(2):
        for s in range(chips):
            kt_scr[part(chip(s), wide), j * rows : (j + 1) * rows] = kv_refs[j * chips + s][0]
            vt_scr[part(chip(s), wide), j * rows : (j + 1) * rows] = kv_refs[j * chips + s][1]
    tokens = level_scr.shape[1]

    def several(j):
        lanes = pl.ds(j, tile)
        units = [(flip, h) for flip in range(2) for h in range(HEADS // 2)]
        heads = [head_group(chips, flip) + h for flip, h in units]
        scores = [
            lax.dot_general(
                kt_scr[part(head, HD), :],
                states[flip][0][h * HD : (h + 1) * HD, lanes],
                TN,
                preferred_element_type=jnp.float32,
            )
            for (flip, h), head in zip(units, heads)
        ]
        olds = [states[flip][2][8 * h : 8 * h + 1, lanes] for flip, h in units]
        tops = [jnp.maximum(jnp.max(s, axis=0, keepdims=True), o) for s, o in zip(scores, olds)]
        weights = [
            jnp.exp2((s - top) * EXP_SCALE).astype(jnp.bfloat16) for s, top in zip(scores, tops)
        ]
        numers = [
            jnp.dot(with_ones(vt_scr[part(head, HD), :]), w, preferred_element_type=jnp.float32)
            for head, w in zip(heads, weights)
        ]
        row = lax.broadcasted_iota(jnp.int32, (8, tile), 0)
        levels = jnp.zeros((8, tile), jnp.float32)
        for (flip, h), head, old_top, top, numer in zip(units, heads, olds, tops, numers):
            old = jnp.exp2((old_top - top) * EXP_SCALE)
            total = numer[HD : HD + 1] + states[flip][3][8 * h : 8 * h + 1, lanes] * old
            inverse = 1.0 / total
            mixed = states[flip][1][h * HD : (h + 1) * HD, lanes] * (old * inverse)
            mixed = mixed + numer[:HD] * inverse
            out_scr[part(head, HD), lanes] = mixed.astype(jnp.bfloat16)
            levels = jnp.where(row == head, top * EXP_SCALE + jnp.log2(total), levels)
        level_scr[:, lanes] = levels

    each_tile(tokens // tile, tile, several)
    level = level_scr[...]
    high = level.astype(jnp.bfloat16)
    rest = level - high.astype(jnp.float32)
    middle = rest.astype(jnp.bfloat16)
    low = rest - middle.astype(jnp.float32)
    stat = jnp.concatenate(
        (high.astype(jnp.float32), middle.astype(jnp.float32), low, jnp.zeros_like(low)), axis=0
    )
    out_scr[WIDTH:, :] = stat.astype(jnp.bfloat16)
    count = tokens // chips
    for s in range(chips):
        out_refs[s][...] = out_scr[:, part(chip(s), count)]


def regroup_kernel(chips, *refs):
    kv_refs, (mine_ref, other_ref) = refs[:chips], refs[chips:]
    wide, slots = kv_refs[0].shape[1], kv_refs[0].shape[2] // 2
    for s in range(chips):
        for i in range(2):
            mine_ref[i, part(chip(s), wide), :] = kv_refs[s][i, :, part(core(0), slots)]
            other_ref[i, part(chip(s), wide), :] = kv_refs[s][i, :, part(core(1), slots)]


def join_kernel(chips, mine_ref, got_ref, nk_ref, nv_ref, scr):
    size = mine_ref.shape[2] // chips
    for i, out_ref in enumerate((nk_ref, nv_ref)):
        for j, ref in enumerate((mine_ref, got_ref)):
            rows = ref[i].astype(jnp.float32).T
            for c in range(chips):
                scr[part(core(j) + 2 * c, size), :] = rows[c * size : (c + 1) * size]
        out_ref[...] = scr[...].astype(jnp.bfloat16)


def finish_kernel(count, *refs):
    got, out_ref = refs[:count], refs[count]
    levels = [rows_to_levels(got[r][WIDTH:, :]) for r in range(count)]
    best = functools.reduce(jnp.maximum, levels)
    factors = [jnp.exp2(level - best) for level in levels]
    inverse = 1.0 / functools.reduce(jnp.add, factors)
    factors = [factor * inverse for factor in factors]
    for h in range(HEADS):
        lo, hi = h * HD, (h + 1) * HD
        mixed = None
        for r in range(count):
            piece = got[r][lo:hi, :].astype(jnp.float32) * factors[r][h : h + 1, :]
            mixed = piece if mixed is None else mixed + piece
        out_ref[:, lo:hi] = mixed.T.astype(jnp.bfloat16)


def body(tokens, query_weight, key_weight, value_weight, cache_keys, cache_values, lengths, assign):
    owners = lax.axis_size("patch")
    shards = lax.axis_size("stream")
    chips = owners // 2
    rows, features = tokens.shape[1:]
    groups = rows // APP
    most = max(2, 2 * groups // owners)
    slots = chips * most * APP
    share = WIDTH // owners
    wide = WIDTH // chips
    half = chips * rows
    depth = query_weight.shape[0]
    cached_rows = cache_keys.shape[1]
    bf16, f32 = jnp.bfloat16, jnp.float32

    def shape(*dims, dtype=bf16):
        return jax.ShapeDtypeStruct(dims, dtype)

    def swap(x, axis, r):
        size = lax.axis_size(axis)
        return lax.ppermute(x, axis, [(i, i ^ r) for i in range(size)])

    def twin(x):
        return swap(x, "patch", 1)

    def far(parts, order=None):
        got = {0: parts[0]}
        for s in order or range(chips - 1, 0, -1):
            got[s] = swap(parts[s], "patch", 2 * s)
        return [got[s] for s in range(chips)]

    normed = call(normalize_kernel, shape(rows, features), (tokens[0],), flops=4 * rows * features)
    x_all = far([normed] * chips)
    wq, wkv = call(
        columns_kernel,
        (shape(share, depth), shape(2 * share, depth)),
        (query_weight, key_weight, value_weight),
        hbm=3,
        scratch=[pltpu.VMEM((3, depth, min(WIDTH, 256)), bf16)],
        sems=[pltpu.SemaphoreType.DMA((3,))],
        flops=6 * share * WIDTH * depth,
        limit=60 << 20,
    )
    wq_all = [wq] + [swap(wq, "stream", s) for s in range(1, shards)]
    wkv_all = [wkv] + [swap(wkv, "stream", s) for s in range(1, shards)]
    other_keys = twin(cache_keys[0])
    other_values = twin(cache_values[0])
    other_length = twin(lengths)
    tgt = call(
        functools.partial(target_kernel, owners, most),
        shape(8, rows, dtype=jnp.int32),
        (assign.reshape(1, groups),),
        flops=1 << 20,
    )
    t_all = far([tgt] * chips)
    kk, vt = call(
        stage_kernel,
        (shape(2, cached_rows, WIDTH), shape(2, WIDTH, cached_rows)),
        (cache_keys[0], cache_values[0], other_keys, other_values),
        hbm=4,
        scratch=[pltpu.VMEM((2, cached_rows, WIDTH), bf16)],
        sems=[pltpu.SemaphoreType.DMA((4,))],
        flops=1 << 20,
    )

    def whole(parts, kinds):
        parts = parts + [twin(p) for p in parts]
        return call(
            functools.partial(gather_weights_kernel, shards, kinds),
            shape(kinds * wide, shards * depth),
            parts,
            scratch=[pltpu.VMEM((kinds * wide, shards * depth), f32)],
            flops=1 << 20,
        )

    wq_full = whole(wq_all, 1)
    q_own, x_full = call(
        functools.partial(project_q_kernel, chips),
        (shape(wide, half), shape(half, features)),
        (*x_all, wq_full),
        flops=2 * wide * half * features,
    )
    near = list(range(1, chips // 2)) + list(range(chips // 2, chips))
    q_all = far([q_own] * chips, order=near)
    wkv_full = whole(wkv_all, 2)
    projected = call(
        functools.partial(project_kv_kernel, chips),
        (shape(2 * wide, half),) + (shape(2, wide, rows),) * chips,
        (x_full, wkv_full),
        flops=4 * wide * half * features,
    )
    kv_own, dense = projected[0], far(projected[1:])
    dense = dense + [twin(d) for d in dense]
    hits = call(
        functools.partial(hits_kernel, chips),
        (shape(2 * slots, half),) * chips,
        t_all,
        scratch=[pltpu.VMEM((8, half), jnp.int32)],
        flops=1 << 20,
    )
    selected = call(
        functools.partial(select_kernel, chips),
        (shape(2, wide, 2 * slots),) * chips,
        (*hits, kv_own),
        flops=8 * wide * half * slots * chips,
    )
    sent = far(selected)
    tile = min(256, half)

    def cached(flip):
        first = flip * (chips // 2)
        return call(
            functools.partial(cached_kernel, chips, flip, tile),
            (
                shape(WIDTH // 2, half),
                shape(WIDTH // 2, half, dtype=f32),
                shape(4 * HEADS, half, dtype=f32),
                shape(4 * HEADS, half, dtype=f32),
            ),
            (lengths[0], other_length[0], *q_all[first : first + chips // 2], kk, vt),
            smem=2,
            flops=4 * cached_rows * half * WIDTH,
        )

    states = [*cached(0), *cached(1)]
    parts = call(
        functools.partial(appended_kernel, chips, min(512, half)),
        (shape(WIDTH + STAT_ROWS, rows),) * chips,
        (*dense, *states),
        scratch=[
            pltpu.VMEM((WIDTH, 2 * rows), bf16),
            pltpu.VMEM((WIDTH, 2 * rows), bf16),
            pltpu.VMEM((WIDTH + STAT_ROWS, half), bf16),
            pltpu.VMEM((8, half), f32),
        ],
        flops=8 * rows * half * WIDTH,
    )
    got = far(parts)
    mine, other = call(
        functools.partial(regroup_kernel, chips), (shape(2, WIDTH, slots),) * 2, sent, flops=1 << 20
    )
    new_keys, new_values = call(
        functools.partial(join_kernel, chips),
        (shape(2 * slots, WIDTH),) * 2,
        (mine, twin(other)),
        scratch=[pltpu.VMEM((2 * slots, WIDTH), f32)],
        flops=1 << 20,
    )
    attended = call(
        functools.partial(finish_kernel, chips),
        shape(rows, WIDTH),
        got,
        flops=4 * chips * rows * WIDTH,
    )
    return attended[None], new_keys[None], new_values[None]


def solution(mesh):
    placed = (
        P("stream", "patch", None),
        P("stream", None),
        P("stream", None),
        P("stream", None),
        P("stream", "patch", None),
        P("stream", "patch", None),
        P("stream", "patch"),
        P("stream", "patch", None),
    )
    return jax.shard_map(
        body,
        mesh=mesh,
        in_specs=placed,
        out_specs=(
            P("stream", "patch", None),
            P("stream", "patch", None),
            P("stream", "patch", None),
        ),
        check_vma=False,
    )
```

time: 305 us -> 108 us (0.35)
  waiting for transfers between devices: 159 us -> 48.7 us
  local copies, waits for them, and re-layouts: 51.4 us -> 0.9 us
  matrix products: 30.4 us -> 0 us
  other arithmetic: 23.7 us -> 0 us
  Pallas kernels: 0 us -> 19.3 us
  starting transfers between devices: 19.5 us -> 37.2 us
  between operations: 13.9 us -> 1.56 us
  loops' own time: 5.28 us -> 0 us
    reduce_scatter x1 -> x0, waiting for transfers between devices: 84.3 us -> none  [body(): lax.psum_scatter(jnp.dot(columns, joined, preferred_element_type=jnp.floa...]
    ppermute x0 -> x40, waiting for transfers between devices: none -> 48.7 us  [swap(): return lax.ppermute(x, axis, [(i, i ^ r) for i in range(size)])]
    all_gather x2 -> x0, waiting for transfers between devices: 39.9 us -> none  [the longest x1 39.8 us: body(): gathered = lax.all_gather(normed, 'stream', axis=0, tiled=True)]
    ppermute x0 -> x40, starting transfers between devices: none -> 37.2 us  [swap(): return lax.ppermute(x, axis, [(i, i ^ r) for i in range(size)])]
    all_to_all x5 -> x0, waiting for transfers between devices: 34.9 us -> none  [the longest x1 18.5 us: body(): lax.all_to_all(numer.reshape(1, -1, width), 'patch', split_axis=1, concat...]
    dot_general x16 -> x0, matrix products: 30.4 us -> none  [the longest x7 13.5 us: fold_block(): jnp.einsum('thd,khd->thk', all_queries, key_rows.reshape(-1, HEADS, HD),...]
    all_to_all x5 -> x0, starting transfers between devices: 19.4 us -> none  [the longest x1 4.19 us: body(): lax.all_to_all(numer.reshape(1, -1, width), 'patch', split_axis=1, concat...]
    pallas_call x0 -> x16, Pallas kernels: none -> 19.3 us  [call(): pl.pallas_call(kernel, out_shape=out_shape, in_specs=[SMEM] * smem + [VME...]
  transfers between devices with their start and end apart: 8 -> 40, of which waited for: 5 -> 14; matrix products, arithmetic and copies ran while one was open for 13% -> 0% of each run, Pallas kernels for 0% -> 15%
where the time goes in v1:
time: 108 us
  waiting for transfers between devices  48.7 us (45%)
  starting transfers between devices  37.2 us (34%)
  Pallas kernels  19.3 us (18%)
  between operations  1.56 us (1%)
    ppermute x40, waiting for transfers between devices, swap(): return lax.ppermute(x, axis, [(i, i ^ r) for i in range(size)])  48.7 us
    ppermute x40, starting transfers between devices, swap(): return lax.ppermute(x, axis, [(i, i ^ r) for i in range(size)])  37.2 us
    pallas_call x16, Pallas kernels, call(): pl.pallas_call(kernel, out_shape=out_shape, in_specs=[SMEM] * smem + [VME...  19.3 us
  transfers between devices with their start and end apart: 40, of which 14 were waited for; matrix products, arithmetic and copies ran while one was open for 0% of the time, Pallas kernels for 15%

profile of v1, /device:TPU:0, one launch (start us, length us, event | category | flops | bytes accessed | tf_op | source)
XLA Modules:
  0.0 107.6 jit_solution(5230241018102759974)
XLA Ops:
  0.7 2.4 %shard_map.104 = (bf16[96,384]{1,0:T(8,128)(2,1)}, bf16[192,384]{1,0:T(8,128)(2,1)}) custom-call(bf16[384,768]{1,0:T(8,128)(2,1)} %wq_ref.1, bf16[384,768]{1,0:T(8,128)(2,1)} %wk_ref.1, bf16[384,768]{1,0:T(8,128)(2,1)} %wv_ref.1), custom_call_target="tpu_custom_call" | custom-call | flops 169869312 | bytes 1048576 | tf_op jit(solution)/shard_map/pallas_call | solution.py:34
  3.0 3.1 %collective-permute-start.3 = (bf16[96,384]{1,0:T(8,128)(2,1)}, bf16[96,384]{1,0:T(8,128)(2,1)S(1)}, u32[]{:S(2)}, u32[]{:S(2)}) collective-permute-start(bf16[96,384]{1,0:T(8,128)(2,1)} %get-tuple-element.38.refs_0_), channel_id=1, source_target_pairs={{0,8},{8,0},{16,24},{24,16},{1,9},{9,1},{17,25},{25,17},{2,10},{10... | collective-permute-start | bytes 221192 | tf_op jit(solution)/shard_map/ppermute | solution.py:401
  6.2 2.6 %collective-permute-start.4 = (bf16[96,384]{1,0:T(8,128)(2,1)}, bf16[96,384]{1,0:T(8,128)(2,1)S(1)}, u32[]{:S(2)}, u32[]{:S(2)}) collective-permute-start(bf16[96,384]{1,0:T(8,128)(2,1)} %get-tuple-element.38.refs_0_), channel_id=1, source_target_pairs={{0,16},{8,24},{16,0},{24,8},{1,17},{9,25},{17,1},{25,9},{2,18},{10... | collective-permute-start | bytes 221192 | tf_op jit(solution)/shard_map/ppermute | solution.py:401
  8.8 0.2 shard_map.114.refs_0_
  9.0 1.7 %collective-permute-start.33 = (s32[8,128]{1,0:T(8,128)S(1)}, s32[8,128]{1,0:T(8,128)S(1)}, u32[]{:S(2)}, u32[]{:S(2)}) collective-permute-start(s32[8,128]{1,0:T(8,128)S(1)} %shard_map.114.refs_0_), channel_id=1, source_target_pairs={{0,2},{1,3},{2,0},{3,1},{4,6},{5,7},{6,4},{7,5},{8,10},{9,11},{10,... | collective-permute-start | bytes 12296 | tf_op jit(solution)/shard_map/ppermute | solution.py:401
  10.7 1.9 %collective-permute-done.33.refs_1_ = s32[8,128]{1,0:T(8,128)S(1)} collective-permute-done((s32[8,128]{1,0:T(8,128)S(1)}, s32[8,128]{1,0:T(8,128)S(1)}, u32[]{:S(2)}, u32[]{:S(2)}) %collective-permute-start.33) | collective-permute-done | bytes 4128 | tf_op jit(solution)/shard_map/ppermute | solution.py:401
  12.6 1.7 %collective-permute-start.34 = (s32[8,128]{1,0:T(8,128)S(1)}, s32[8,128]{1,0:T(8,128)S(1)}, u32[]{:S(2)}, u32[]{:S(2)}) collective-permute-start(s32[8,128]{1,0:T(8,128)S(1)} %shard_map.114.refs_0_), channel_id=1, source_target_pairs={{0,4},{1,5},{2,6},{3,7},{4,0},{5,1},{6,2},{7,3},{8,12},{9,13},{10,... | collective-permute-start | bytes 12296 | tf_op jit(solution)/shard_map/ppermute | solution.py:401
  14.4 1.9 %collective-permute-done.34.refs_2_ = s32[8,128]{1,0:T(8,128)S(1)} collective-permute-done((s32[8,128]{1,0:T(8,128)S(1)}, s32[8,128]{1,0:T(8,128)S(1)}, u32[]{:S(2)}, u32[]{:S(2)}) %collective-permute-start.34) | collective-permute-done | bytes 4128 | tf_op jit(solution)/shard_map/ppermute | solution.py:401
  16.2 2.7 %collective-permute-start.35 = (s32[8,128]{1,0:T(8,128)S(1)}, s32[8,128]{1,0:T(8,128)S(1)}, u32[]{:S(2)}, u32[]{:S(2)}) collective-permute-start(s32[8,128]{1,0:T(8,128)S(1)} %shard_map.114.refs_0_), channel_id=1, source_target_pairs={{0,6},{1,7},{2,4},{3,5},{4,2},{5,3},{6,0},{7,1},{8,14},{9,15},{10,... | collective-permute-start | bytes 12296 | tf_op jit(solution)/shard_map/ppermute | solution.py:401
  18.9 1.8 %collective-permute-done.35.refs_3_ = s32[8,128]{1,0:T(8,128)S(1)} collective-permute-done((s32[8,128]{1,0:T(8,128)S(1)}, s32[8,128]{1,0:T(8,128)S(1)}, u32[]{:S(2)}, u32[]{:S(2)}) %collective-permute-start.35) | collective-permute-done | bytes 4128 | tf_op jit(solution)/shard_map/ppermute | solution.py:401
  20.7 0.9 collective-permute-start.10
  21.6 0.5 collective-permute-start.8
  22.1 0.1 collective-permute-start.9
  22.2 0.4 collective-permute-start.26
  22.7 0.2 collective-permute-done.7.refs_5_
  22.9 3.5 %collective-permute-start.11 = (bf16[192,384]{1,0:T(8,128)(2,1)}, bf16[192,384]{1,0:T(8,128)(2,1)S(1)}, u32[]{:S(2)}, u32[]{:S(2)}) collective-permute-start(bf16[192,384]{1,0:T(8,128)(2,1)} %get-tuple-element.40.refs_0_), channel_id=1, source_target_pairs={{0,16},{8,24},{16,0},{24,8},{1,17},{9,25},{17,1},{25,9},{2,18},{10... | collective-permute-start | bytes 442376 | tf_op jit(solution)/shard_map/ppermute | solution.py:401
  26.4 0.1 collective-permute-start.13
  26.5 0.5 collective-permute-start.27
  27.0 10.2 %collective-permute-done.11.refs_2_ = bf16[192,384]{1,0:T(8,128)(2,1)S(1)} collective-permute-done((bf16[192,384]{1,0:T(8,128)(2,1)}, bf16[192,384]{1,0:T(8,128)(2,1)S(1)}, u32[]{:S(2)}, u32[]{:S(2)}) %collective-permute-start.11) | collective-permute-done | bytes 147488 | tf_op jit(solution)/shard_map/ppermute | solution.py:401
  37.2 0.5 collective-permute-start.15
  37.7 0.1 collective-permute-start.16
  37.8 0.2 shard_map.103.refs_0_
  38.0 0.6 collective-permute-done.14.refs_5_
  38.6 1.6 %collective-permute-start = (bf16[128,1536]{1,0:T(8,128)(2,1)S(1)}, bf16[128,1536]{1,0:T(8,128)(2,1)S(1)}, u32[]{:S(2)}, u32[]{:S(2)}) collective-permute-start(bf16[128,1536]{1,0:T(8,128)(2,1)S(1)} %shard_map.103.refs_0_), channel_id=1, source_target_pairs={{0,2},{1,3},{2,0},{3,1},{4,6},{5,7},{6,4},{7,5},{8,10},{9,11},{10,... | collective-permute-start | bytes 1179656 | tf_op jit(solution)/shard_map/ppermute | solution.py:401
  40.2 1.5 %collective-permute-start.1 = (bf16[128,1536]{1,0:T(8,128)(2,1)S(1)}, bf16[128,1536]{1,0:T(8,128)(2,1)S(1)}, u32[]{:S(2)}, u32[]{:S(2)}) collective-permute-start(bf16[128,1536]{1,0:T(8,128)(2,1)S(1)} %shard_map.103.refs_0_), channel_id=1, source_target_pairs={{0,4},{1,5},{2,6},{3,7},{4,0},{5,1},{6,2},{7,3},{8,12},{9,13},{10,... | collective-permute-start | bytes 1179656 | tf_op jit(solution)/shard_map/ppermute | solution.py:401
  41.7 0.4 collective-permute-start.2
  42.1 0.4 shard_map.115
  42.5 0.9 copy-done.4
  43.4 0.1 shard_map.105.refs_4_
  43.6 0.3 shard_map.107.w_ref
  43.8 6.7 %collective-permute-done.refs_1_ = bf16[128,1536]{1,0:T(8,128)(2,1)S(1)} collective-permute-done((bf16[128,1536]{1,0:T(8,128)(2,1)S(1)}, bf16[128,1536]{1,0:T(8,128)(2,1)S(1)}, u32[]{:S(2)}, u32[]{:S(2)}) %collective-permute-start) | collective-permute-done | bytes 393248 | tf_op jit(solution)/shard_map/ppermute | solution.py:401
  50.6 8.9 %collective-permute-done.1.refs_2_ = bf16[128,1536]{1,0:T(8,128)(2,1)S(1)} collective-permute-done((bf16[128,1536]{1,0:T(8,128)(2,1)S(1)}, bf16[128,1536]{1,0:T(8,128)(2,1)S(1)}, u32[]{:S(2)}, u32[]{:S(2)}) %collective-permute-start.1) | collective-permute-done | bytes 393248 | tf_op jit(solution)/shard_map/ppermute | solution.py:401
  59.5 0.8 shard_map.106
  60.3 0.9 shard_map.108
  61.2 0.6 shard_map.116
  61.8 1.3 %collective-permute-start.36 = (bf16[2,192,256]{2,1,0:T(8,128)(2,1)S(1)}, bf16[2,192,256]{2,1,0:T(8,128)(2,1)S(1)}, u32[]{:S(2)}, u32[]{:S(2)}) collective-permute-start(bf16[2,192,256]{2,1,0:T(8,128)(2,1)S(1)} %get-tuple-element.66), channel_id=1, source_target_pairs={{0,2},{1,3},{2,0},{3,1},{4,6},{5,7},{6,4},{7,5},{8,10},{9,11},{10,... | collective-permute-start | bytes 589832 | tf_op jit(solution)/shard_map/ppermute | solution.py:401
  63.1 0.9 collective-permute-start.37
  64.1 1.3 %collective-permute-start.38 = (bf16[2,192,256]{2,1,0:T(8,128)(2,1)S(1)}, bf16[2,192,256]{2,1,0:T(8,128)(2,1)S(1)}, u32[]{:S(2)}, u32[]{:S(2)}) collective-permute-start(bf16[2,192,256]{2,1,0:T(8,128)(2,1)S(1)} %get-tuple-element.68), channel_id=1, source_target_pairs={{0,6},{1,7},{2,4},{3,5},{4,2},{5,3},{6,0},{7,1},{8,14},{9,15},{10,... | collective-permute-start | bytes 589832 | tf_op jit(solution)/shard_map/ppermute | solution.py:401
  65.4 4.2 %collective-permute-done.36.refs_1_ = bf16[2,192,256]{2,1,0:T(8,128)(2,1)S(1)} collective-permute-done((bf16[2,192,256]{2,1,0:T(8,128)(2,1)S(1)}, bf16[2,192,256]{2,1,0:T(8,128)(2,1)S(1)}, u32[]{:S(2)}, u32[]{:S(2)}) %collective-permute-start.36) | collective-permute-done | bytes 196640 | tf_op jit(solution)/shard_map/ppermute | solution.py:401
  69.6 1.3 %collective-permute-start.25 = (bf16[192,512]{1,0:T(8,128)(2,1)S(1)}, bf16[192,512]{1,0:T(8,128)(2,1)S(1)}, u32[]{:S(2)}, u32[]{:S(2)}) collective-permute-start(bf16[192,512]{1,0:T(8,128)(2,1)S(1)} %get-tuple-element.45.refs_0_), channel_id=1, source_target_pairs={{0,2},{1,3},{2,0},{3,1},{4,6},{5,7},{6,4},{7,5},{8,10},{9,11},{10,... | collective-permute-start | bytes 589832 | tf_op jit(solution)/shard_map/ppermute | solution.py:401
  70.9 0.6 collective-permute-done.37.refs_2_
  71.5 0.8 collective-permute-start.17
  72.3 2.6 %collective-permute-done.38.refs_3_ = bf16[2,192,256]{2,1,0:T(8,128)(2,1)S(1)} collective-permute-done((bf16[2,192,256]{2,1,0:T(8,128)(2,1)S(1)}, bf16[2,192,256]{2,1,0:T(8,128)(2,1)S(1)}, u32[]{:S(2)}, u32[]{:S(2)}) %collective-permute-start.38) | collective-permute-done | bytes 196640 | tf_op jit(solution)/shard_map/ppermute | solution.py:401
  74.8 0.4 collective-permute-start.28
  75.3 1.4 %collective-permute-start.29 = (bf16[192,512]{1,0:T(8,128)(2,1)S(1)}, bf16[192,512]{1,0:T(8,128)(2,1)S(1)}, u32[]{:S(2)}, u32[]{:S(2)}) collective-permute-start(bf16[192,512]{1,0:T(8,128)(2,1)S(1)} %get-tuple-element.45.refs_0_), channel_id=1, source_target_pairs={{0,6},{1,7},{2,4},{3,5},{4,2},{5,3},{6,0},{7,1},{8,14},{9,15},{10,... | collective-permute-start | bytes 589832 | tf_op jit(solution)/shard_map/ppermute | solution.py:401
  77.4 0.1 shard_map.117
  77.5 0.1 collective-permute-start.24
  77.6 1.8 %shard_map.109 = (bf16[2,768,768]{2,1,0:T(8,128)(2,1)S(1)}, bf16[2,768,768]{2,1,0:T(8,128)(2,1)S(1)}) custom-call(bf16[768,768]{1,0:T(8,128)(2,1)S(1)} %bitcast.12, bf16[768,768]{1,0:T(8,128)(2,1)S(1)} %bitcast.14, bf16[768,768]{1,0:T(8,128)(2,1)S(1)} %collective-permute-done.26.k1_ref, bf16[768,768]{1,0:T(8,128)(2,1)S(1)} %collective-permute-done.27.v1_ref), custom_call_target="tpu_custom_call" | custom-call | flops 1048576 | bytes 1048576 | tf_op jit(solution)/shard_map/pallas_call | solution.py:34
  79.4 1.4 %collective-permute-start.18 = (bf16[2,192,128]{2,1,0:T(8,128)(2,1)S(1)}, bf16[2,192,128]{2,1,0:T(8,128)(2,1)S(1)}, u32[]{:S(2)}, u32[]{:S(2)}) collective-permute-start(bf16[2,192,128]{2,1,0:T(8,128)(2,1)S(1)} %get-tuple-element.43), channel_id=1, source_target_pairs={{0,4},{1,5},{2,6},{3,7},{4,0},{5,1},{6,2},{7,3},{8,12},{9,13},{10,... | collective-permute-start | bytes 294920 | tf_op jit(solution)/shard_map/ppermute | solution.py:401
  80.8 1.8 %collective-permute-start.19 = (bf16[2,192,128]{2,1,0:T(8,128)(2,1)S(1)}, bf16[2,192,128]{2,1,0:T(8,128)(2,1)S(1)}, u32[]{:S(2)}, u32[]{:S(2)}) collective-permute-start(bf16[2,192,128]{2,1,0:T(8,128)(2,1)S(1)} %get-tuple-element.44), channel_id=1, source_target_pairs={{0,6},{1,7},{2,4},{3,5},{4,2},{5,3},{6,0},{7,1},{8,14},{9,15},{10,... | collective-permute-start | bytes 294920 | tf_op jit(solution)/shard_map/ppermute | solution.py:401
  82.6 3.7 %shard_map.110 = (bf16[384,512]{1,0:T(8,128)(2,1)S(1)}, f32[384,512]{1,0:T(8,128)S(1)}, f32[24,512]{1,0:T(8,128)S(1)}, f32[24,512]{1,0:T(8,128)S(1)}) custom-call(s32[1]{0:T(128)} %bitcast.9.len0_ref, s32[1]{0:T(128)} %bitcast.2.len1_ref, bf16[192,512]{1,0:T(8,128)(2,1)S(1)} %get-tuple-element.45.refs_0_, ...), custom_call_target="tpu_custom_call" | custom-call | flops 1207959552 | bytes 1048576 | tf_op jit(solution)/shard_map/pallas_call | solution.py:34
  86.2 2.1 %collective-permute-done.18.refs_2_ = bf16[2,192,128]{2,1,0:T(8,128)(2,1)S(1)} collective-permute-done((bf16[2,192,128]{2,1,0:T(8,128)(2,1)S(1)}, bf16[2,192,128]{2,1,0:T(8,128)(2,1)S(1)}, u32[]{:S(2)}, u32[]{:S(2)}) %collective-permute-start.18) | collective-permute-done | bytes 98336 | tf_op jit(solution)/shard_map/ppermute | solution.py:401
  88.4 0.5 collective-permute-start.21
  88.9 0.1 collective-permute-start.22
  89.0 0.4 collective-permute-start.23
  89.4 3.8 %shard_map.111 = (bf16[384,512]{1,0:T(8,128)(2,1)S(1)}, f32[384,512]{1,0:T(8,128)S(1)}, f32[24,512]{1,0:T(8,128)S(1)}, f32[24,512]{1,0:T(8,128)S(1)}) custom-call(s32[1]{0:T(128)} %bitcast.10.len0_ref, s32[1]{0:T(128)} %bitcast.2.len1_ref, bf16[192,512]{1,0:T(8,128)(2,1)S(1)} %collective-permute-done.28.refs_0_, ...), custom_call_target="tpu_custom_call" | custom-call | flops 1207959552 | bytes 1048576 | tf_op jit(solution)/shard_map/pallas_call | solution.py:34
  93.3 1.8 %shard_map.112 = (bf16[800,128]{1,0:T(8,128)(2,1)S(1)}, bf16[800,128]{1,0:T(8,128)(2,1)S(1)}, bf16[800,128]{1,0:T(8,128)(2,1)S(1)}, bf16[800,128]{1,0:T(8,128)(2,1)S(1)}) custom-call(bf16[2,192,128]{2,1,0:T(8,128)(2,1)S(1)} %get-tuple-element.41.refs_0_, bf16[2,192,128]{2,1,0:T(8,128)(2,1)S(1)} %collective-permute-done.17.refs_1_, ...), custom_call_target="tpu_custom_call" | custom-call | flops 402653184 | bytes 1048576 | tf_op jit(solution)/shard_map/pallas_call | solution.py:34
  95.1 0.1 collective-permute-start.30
  95.1 2.0 %collective-permute-start.31 = (bf16[800,128]{1,0:T(8,128)(2,1)S(1)}, bf16[800,128]{1,0:T(8,128)(2,1)S(1)}, u32[]{:S(2)}, u32[]{:S(2)}) collective-permute-start(bf16[800,128]{1,0:T(8,128)(2,1)S(1)} %get-tuple-element.58), channel_id=1, source_target_pairs={{0,4},{1,5},{2,6},{3,7},{4,0},{5,1},{6,2},{7,3},{8,12},{9,13},{10,... | collective-permute-start | bytes 614408 | tf_op jit(solution)/shard_map/ppermute | solution.py:401
  97.1 1.5 %collective-permute-start.32 = (bf16[800,128]{1,0:T(8,128)(2,1)S(1)}, bf16[800,128]{1,0:T(8,128)(2,1)S(1)}, u32[]{:S(2)}, u32[]{:S(2)}) collective-permute-start(bf16[800,128]{1,0:T(8,128)(2,1)S(1)} %get-tuple-element.59), channel_id=1, source_target_pairs={{0,6},{1,7},{2,4},{3,5},{4,2},{5,3},{6,0},{7,1},{8,14},{9,15},{10,... | collective-permute-start | bytes 614408 | tf_op jit(solution)/shard_map/ppermute | solution.py:401
  98.6 1.2 %shard_map.118 = (bf16[256,768]{1,0:T(8,128)(2,1)}, bf16[256,768]{1,0:T(8,128)(2,1)}) custom-call(bf16[2,768,128]{2,1,0:T(8,128)(2,1)S(1)} %get-tuple-element.69.mine_ref, bf16[2,768,128]{2,1,0:T(8,128)(2,1)S(1)} %collective-permute-done.39.got_ref), custom_call_target="tpu_custom_call" | custom-call | flops 1048576 | bytes 1048576 | tf_op jit(solution)/shard_map/pallas_call | solution.py:34
  99.9 3.2 %collective-permute-done.30.refs_1_ = bf16[800,128]{1,0:T(8,128)(2,1)S(1)} collective-permute-done((bf16[800,128]{1,0:T(8,128)(2,1)S(1)}, bf16[800,128]{1,0:T(8,128)(2,1)S(1)}, u32[]{:S(2)}, u32[]{:S(2)}) %collective-permute-start.30) | collective-permute-done | bytes 204832 | tf_op jit(solution)/shard_map/ppermute | solution.py:401
  103.1 3.5 %collective-permute-done.31.refs_2_ = bf16[800,128]{1,0:T(8,128)(2,1)S(1)} collective-permute-done((bf16[800,128]{1,0:T(8,128)(2,1)S(1)}, bf16[800,128]{1,0:T(8,128)(2,1)S(1)}, u32[]{:S(2)}, u32[]{:S(2)}) %collective-permute-start.31) | collective-permute-done | bytes 204832 | tf_op jit(solution)/shard_map/ppermute | solution.py:401
  106.6 0.9 shard_map.113
  (44 shorter events, 0.1 us)
Async XLA Ops:
  0.6 8.1 %copy-start.5 = (s32[1,32,1]{1,2,0:T(1,128)S(1)}, s32[1,32,1]{1,2,0:T(1,128)}, u32[]{:S(2)}) copy-start(s32[1,32,1]{1,2,0:T(1,128)} %param.15) | copy-start | bytes 388
  0.6 21.6 %copy-start = (bf16[1,768,768]{2,1,0:T(8,128)(2,1)S(1)}, bf16[1,768,768]{2,1,0:T(8,128)(2,1)}, u32[]{:S(2)}) copy-start(bf16[1,768,768]{2,1,0:T(8,128)(2,1)} %param.12) | copy-start | bytes 3538948
  0.7 37.2 %copy-start.2 = (bf16[1,128,1536]{2,1,0:T(8,128)(2,1)S(1)}, bf16[1,128,1536]{2,1,0:T(8,128)(2,1)}, u32[]{:S(2)}) copy-start(bf16[1,128,1536]{2,1,0:T(8,128)(2,1)} %param.8) | copy-start | bytes 1179652
  3.0 40.5 %copy-start.3 = (bf16[192,384]{1,0:T(8,128)(2,1)S(1)}, bf16[192,384]{1,0:T(8,128)(2,1)}, u32[]{:S(2)}) copy-start(bf16[192,384]{1,0:T(8,128)(2,1)} %get-tuple-element.40.refs_0_) | copy-start | bytes 442372
  3.0 18.6 %collective-permute-start.3 = (bf16[96,384]{1,0:T(8,128)(2,1)}, bf16[96,384]{1,0:T(8,128)(2,1)S(1)}, u32[]{:S(2)}, u32[]{:S(2)}) collective-permute-start(bf16[96,384]{1,0:T(8,128)(2,1)} %get-tuple-element.38.refs_0_), channel_id=1, source_target_pairs={{0,8},{8,0},{16,24},{24,16},{1,9},{9,1},{17,25},{25,17},{2,10},{10... | collective-permute-start | bytes 221192 | tf_op jit(solution)/shard_map/ppermute | solution.py:401
  6.2 15.5 %collective-permute-start.4 = (bf16[96,384]{1,0:T(8,128)(2,1)}, bf16[96,384]{1,0:T(8,128)(2,1)S(1)}, u32[]{:S(2)}, u32[]{:S(2)}) collective-permute-start(bf16[96,384]{1,0:T(8,128)(2,1)} %get-tuple-element.38.refs_0_), channel_id=1, source_target_pairs={{0,16},{8,24},{16,0},{24,8},{1,17},{9,25},{17,1},{25,9},{2,18},{10... | collective-permute-start | bytes 221192 | tf_op jit(solution)/shard_map/ppermute | solution.py:401
  8.8 13.4 %collective-permute-start.5 = (bf16[96,384]{1,0:T(8,128)(2,1)}, bf16[96,384]{1,0:T(8,128)(2,1)S(1)}, u32[]{:S(2)}, u32[]{:S(2)}) collective-permute-start(bf16[96,384]{1,0:T(8,128)(2,1)} %get-tuple-element.38.refs_0_), channel_id=1, source_target_pairs={{0,24},{8,16},{16,8},{24,0},{1,25},{9,17},{17,9},{25,1},{2,26},{10... | collective-permute-start | bytes 221192 | tf_op jit(solution)/shard_map/ppermute | solution.py:401
  9.0 3.6 %collective-permute-start.33 = (s32[8,128]{1,0:T(8,128)S(1)}, s32[8,128]{1,0:T(8,128)S(1)}, u32[]{:S(2)}, u32[]{:S(2)}) collective-permute-start(s32[8,128]{1,0:T(8,128)S(1)} %shard_map.114.refs_0_), channel_id=1, source_target_pairs={{0,2},{1,3},{2,0},{3,1},{4,6},{5,7},{6,4},{7,5},{8,10},{9,11},{10,... | collective-permute-start | bytes 12296 | tf_op jit(solution)/shard_map/ppermute | solution.py:401
  10.7 11.5 %collective-permute-start.6 = (bf16[96,384]{1,0:T(8,128)(2,1)}, bf16[96,384]{1,0:T(8,128)(2,1)S(1)}, u32[]{:S(2)}, u32[]{:S(2)}) collective-permute-start(bf16[96,384]{1,0:T(8,128)(2,1)} %get-tuple-element.38.refs_0_), channel_id=1, source_target_pairs={{0,1},{1,0},{2,3},{3,2},{4,5},{5,4},{6,7},{7,6},{8,9},{9,8},{10,11... | collective-permute-start | bytes 221192 | tf_op jit(solution)/shard_map/ppermute | solution.py:401
  12.6 3.6 %collective-permute-start.34 = (s32[8,128]{1,0:T(8,128)S(1)}, s32[8,128]{1,0:T(8,128)S(1)}, u32[]{:S(2)}, u32[]{:S(2)}) collective-permute-start(s32[8,128]{1,0:T(8,128)S(1)} %shard_map.114.refs_0_), channel_id=1, source_target_pairs={{0,4},{1,5},{2,6},{3,7},{4,0},{5,1},{6,2},{7,3},{8,12},{9,13},{10,... | collective-permute-start | bytes 12296 | tf_op jit(solution)/shard_map/ppermute | solution.py:401
  16.2 4.5 %collective-permute-start.35 = (s32[8,128]{1,0:T(8,128)S(1)}, s32[8,128]{1,0:T(8,128)S(1)}, u32[]{:S(2)}, u32[]{:S(2)}) collective-permute-start(s32[8,128]{1,0:T(8,128)S(1)} %shard_map.114.refs_0_), channel_id=1, source_target_pairs={{0,6},{1,7},{2,4},{3,5},{4,2},{5,3},{6,0},{7,1},{8,14},{9,15},{10,... | collective-permute-start | bytes 12296 | tf_op jit(solution)/shard_map/ppermute | solution.py:401
  20.7 5.7 %collective-permute-start.10 = (bf16[192,384]{1,0:T(8,128)(2,1)}, bf16[192,384]{1,0:T(8,128)(2,1)S(1)}, u32[]{:S(2)}, u32[]{:S(2)}) collective-permute-start(bf16[192,384]{1,0:T(8,128)(2,1)} %get-tuple-element.40.refs_0_), channel_id=1, source_target_pairs={{0,8},{8,0},{16,24},{24,16},{1,9},{9,1},{17,25},{25,17},{2,10},{10... | collective-permute-start | bytes 442376 | tf_op jit(solution)/shard_map/ppermute | solution.py:401
  21.6 1.3 %collective-permute-start.7 = (bf16[96,384]{1,0:T(8,128)(2,1)S(1)}, bf16[96,384]{1,0:T(8,128)(2,1)S(1)}, u32[]{:S(2)}, u32[]{:S(2)}) collective-permute-start(bf16[96,384]{1,0:T(8,128)(2,1)S(1)} %collective-permute-done.3.refs_1_), channel_id=1, source_target_pairs={{0,1},{1,0},{2,3},{3,2},{4,5},{5,4},{6,7},{7,6},{8,9},{9,8},{10,11... | collective-permute-start | bytes 221192 | tf_op jit(solution)/shard_map/ppermute | solution.py:401
  21.6 4.8 %collective-permute-start.8 = (bf16[96,384]{1,0:T(8,128)(2,1)S(1)}, bf16[96,384]{1,0:T(8,128)(2,1)S(1)}, u32[]{:S(2)}, u32[]{:S(2)}) collective-permute-start(bf16[96,384]{1,0:T(8,128)(2,1)S(1)} %collective-permute-done.4.refs_2_), channel_id=1, source_target_pairs={{0,1},{1,0},{2,3},{3,2},{4,5},{5,4},{6,7},{7,6},{8,9},{9,8},{10,11... | collective-permute-start | bytes 221192 | tf_op jit(solution)/shard_map/ppermute | solution.py:401
  22.1 4.2 %collective-permute-start.9 = (bf16[96,384]{1,0:T(8,128)(2,1)S(1)}, bf16[96,384]{1,0:T(8,128)(2,1)S(1)}, u32[]{:S(2)}, u32[]{:S(2)}) collective-permute-start(bf16[96,384]{1,0:T(8,128)(2,1)S(1)} %collective-permute-done.5.refs_3_), channel_id=1, source_target_pairs={{0,1},{1,0},{2,3},{3,2},{4,5},{5,4},{6,7},{7,6},{8,9},{9,8},{10,11... | collective-permute-start | bytes 221192 | tf_op jit(solution)/shard_map/ppermute | solution.py:401
  22.2 53.1 %collective-permute-start.26 = (bf16[768,768]{1,0:T(8,128)(2,1)S(1)}, bf16[768,768]{1,0:T(8,128)(2,1)S(1)}, u32[]{:S(2)}, u32[]{:S(2)}) collective-permute-start(bf16[768,768]{1,0:T(8,128)(2,1)S(1)} %bitcast.11), channel_id=1, source_target_pairs={{0,1},{1,0},{2,3},{3,2},{4,5},{5,4},{6,7},{7,6},{8,9},{9,8},{10,11... | collective-permute-start | bytes 3538952 | tf_op jit(solution)/shard_map/ppermute | solution.py:401
  22.9 14.3 %collective-permute-start.11 = (bf16[192,384]{1,0:T(8,128)(2,1)}, bf16[192,384]{1,0:T(8,128)(2,1)S(1)}, u32[]{:S(2)}, u32[]{:S(2)}) collective-permute-start(bf16[192,384]{1,0:T(8,128)(2,1)} %get-tuple-element.40.refs_0_), channel_id=1, source_target_pairs={{0,16},{8,24},{16,0},{24,8},{1,17},{9,25},{17,1},{25,9},{2,18},{10... | collective-permute-start | bytes 442376 | tf_op jit(solution)/shard_map/ppermute | solution.py:401
  26.4 10.8 %collective-permute-start.12 = (bf16[192,384]{1,0:T(8,128)(2,1)}, bf16[192,384]{1,0:T(8,128)(2,1)S(1)}, u32[]{:S(2)}, u32[]{:S(2)}) collective-permute-start(bf16[192,384]{1,0:T(8,128)(2,1)} %get-tuple-element.40.refs_0_), channel_id=1, source_target_pairs={{0,24},{8,16},{16,8},{24,0},{1,25},{9,17},{17,9},{25,1},{2,26},{10... | collective-permute-start | bytes 442376 | tf_op jit(solution)/shard_map/ppermute | solution.py:401
  26.4 11.3 %collective-permute-start.13 = (bf16[192,384]{1,0:T(8,128)(2,1)}, bf16[192,384]{1,0:T(8,128)(2,1)S(1)}, u32[]{:S(2)}, u32[]{:S(2)}) collective-permute-start(bf16[192,384]{1,0:T(8,128)(2,1)} %get-tuple-element.40.refs_0_), channel_id=1, source_target_pairs={{0,1},{1,0},{2,3},{3,2},{4,5},{5,4},{6,7},{7,6},{8,9},{9,8},{10,11... | collective-permute-start | bytes 442376 | tf_op jit(solution)/shard_map/ppermute | solution.py:401
  26.5 51.0 %collective-permute-start.27 = (bf16[768,768]{1,0:T(8,128)(2,1)}, bf16[768,768]{1,0:T(8,128)(2,1)S(1)}, u32[]{:S(2)}, u32[]{:S(2)}) collective-permute-start(bf16[768,768]{1,0:T(8,128)(2,1)} %bitcast.13), channel_id=1, source_target_pairs={{0,1},{1,0},{2,3},{3,2},{4,5},{5,4},{6,7},{7,6},{8,9},{9,8},{10,11... | collective-permute-start | bytes 3538952 | tf_op jit(solution)/shard_map/ppermute | solution.py:401
  37.2 1.4 %collective-permute-start.14 = (bf16[192,384]{1,0:T(8,128)(2,1)S(1)}, bf16[192,384]{1,0:T(8,128)(2,1)S(1)}, u32[]{:S(2)}, u32[]{:S(2)}) collective-permute-start(bf16[192,384]{1,0:T(8,128)(2,1)S(1)} %collective-permute-done.10.refs_1_), channel_id=1, source_target_pairs={{0,1},{1,0},{2,3},{3,2},{4,5},{5,4},{6,7},{7,6},{8,9},{9,8},{10,11... | collective-permute-start | bytes 442376 | tf_op jit(solution)/shard_map/ppermute | solution.py:401
  37.2 3.0 %collective-permute-start.15 = (bf16[192,384]{1,0:T(8,128)(2,1)S(1)}, bf16[192,384]{1,0:T(8,128)(2,1)S(1)}, u32[]{:S(2)}, u32[]{:S(2)}) collective-permute-start(bf16[192,384]{1,0:T(8,128)(2,1)S(1)} %collective-permute-done.11.refs_2_), channel_id=1, source_target_pairs={{0,1},{1,0},{2,3},{3,2},{4,5},{5,4},{6,7},{7,6},{8,9},{9,8},{10,11... | collective-permute-start | bytes 442376 | tf_op jit(solution)/shard_map/ppermute | solution.py:401
  37.7 4.0 %collective-permute-start.16 = (bf16[192,384]{1,0:T(8,128)(2,1)S(1)}, bf16[192,384]{1,0:T(8,128)(2,1)S(1)}, u32[]{:S(2)}, u32[]{:S(2)}) collective-permute-start(bf16[192,384]{1,0:T(8,128)(2,1)S(1)} %collective-permute-done.12.refs_3_), channel_id=1, source_target_pairs={{0,1},{1,0},{2,3},{3,2},{4,5},{5,4},{6,7},{7,6},{8,9},{9,8},{10,11... | collective-permute-start | bytes 442376 | tf_op jit(solution)/shard_map/ppermute | solution.py:401
  38.6 12.0 %collective-permute-start = (bf16[128,1536]{1,0:T(8,128)(2,1)S(1)}, bf16[128,1536]{1,0:T(8,128)(2,1)S(1)}, u32[]{:S(2)}, u32[]{:S(2)}) collective-permute-start(bf16[128,1536]{1,0:T(8,128)(2,1)S(1)} %shard_map.103.refs_0_), channel_id=1, source_target_pairs={{0,2},{1,3},{2,0},{3,1},{4,6},{5,7},{6,4},{7,5},{8,10},{9,11},{10,... | collective-permute-start | bytes 1179656 | tf_op jit(solution)/shard_map/ppermute | solution.py:401
  40.2 19.3 %collective-permute-start.1 = (bf16[128,1536]{1,0:T(8,128)(2,1)S(1)}, bf16[128,1536]{1,0:T(8,128)(2,1)S(1)}, u32[]{:S(2)}, u32[]{:S(2)}) collective-permute-start(bf16[128,1536]{1,0:T(8,128)(2,1)S(1)} %shard_map.103.refs_0_), channel_id=1, source_target_pairs={{0,4},{1,5},{2,6},{3,7},{4,0},{5,1},{6,2},{7,3},{8,12},{9,13},{10,... | collective-permute-start | bytes 1179656 | tf_op jit(solution)/shard_map/ppermute | solution.py:401
  41.7 17.8 %collective-permute-start.2 = (bf16[128,1536]{1,0:T(8,128)(2,1)S(1)}, bf16[128,1536]{1,0:T(8,128)(2,1)S(1)}, u32[]{:S(2)}, u32[]{:S(2)}) collective-permute-start(bf16[128,1536]{1,0:T(8,128)(2,1)S(1)} %shard_map.103.refs_0_), channel_id=1, source_target_pairs={{0,6},{1,7},{2,4},{3,5},{4,2},{5,3},{6,0},{7,1},{8,14},{9,15},{10,... | collective-permute-start | bytes 1179656 | tf_op jit(solution)/shard_map/ppermute | solution.py:401
  42.5 0.9 copy-start.4
  61.2 16.4 %copy-start.1 = (bf16[1,768,768]{2,1,0:T(8,128)(2,1)S(1)}, bf16[1,768,768]{2,1,0:T(8,128)(2,1)}, u32[]{:S(2)}) copy-start(bf16[1,768,768]{2,1,0:T(8,128)(2,1)} %param.13) | copy-start | bytes 3538948
  61.8 7.8 %collective-permute-start.36 = (bf16[2,192,256]{2,1,0:T(8,128)(2,1)S(1)}, bf16[2,192,256]{2,1,0:T(8,128)(2,1)S(1)}, u32[]{:S(2)}, u32[]{:S(2)}) collective-permute-start(bf16[2,192,256]{2,1,0:T(8,128)(2,1)S(1)} %get-tuple-element.66), channel_id=1, source_target_pairs={{0,2},{1,3},{2,0},{3,1},{4,6},{5,7},{6,4},{7,5},{8,10},{9,11},{10,... | collective-permute-start | bytes 589832 | tf_op jit(solution)/shard_map/ppermute | solution.py:401
  63.1 8.3 %collective-permute-start.37 = (bf16[2,192,256]{2,1,0:T(8,128)(2,1)S(1)}, bf16[2,192,256]{2,1,0:T(8,128)(2,1)S(1)}, u32[]{:S(2)}, u32[]{:S(2)}) collective-permute-start(bf16[2,192,256]{2,1,0:T(8,128)(2,1)S(1)} %get-tuple-element.67), channel_id=1, source_target_pairs={{0,4},{1,5},{2,6},{3,7},{4,0},{5,1},{6,2},{7,3},{8,12},{9,13},{10,... | collective-permute-start | bytes 589832 | tf_op jit(solution)/shard_map/ppermute | solution.py:401
  64.1 10.8 %collective-permute-start.38 = (bf16[2,192,256]{2,1,0:T(8,128)(2,1)S(1)}, bf16[2,192,256]{2,1,0:T(8,128)(2,1)S(1)}, u32[]{:S(2)}, u32[]{:S(2)}) collective-permute-start(bf16[2,192,256]{2,1,0:T(8,128)(2,1)S(1)} %get-tuple-element.68), channel_id=1, source_target_pairs={{0,6},{1,7},{2,4},{3,5},{4,2},{5,3},{6,0},{7,1},{8,14},{9,15},{10,... | collective-permute-start | bytes 589832 | tf_op jit(solution)/shard_map/ppermute | solution.py:401
  69.6 12.9 %collective-permute-start.25 = (bf16[192,512]{1,0:T(8,128)(2,1)S(1)}, bf16[192,512]{1,0:T(8,128)(2,1)S(1)}, u32[]{:S(2)}, u32[]{:S(2)}) collective-permute-start(bf16[192,512]{1,0:T(8,128)(2,1)S(1)} %get-tuple-element.45.refs_0_), channel_id=1, source_target_pairs={{0,2},{1,3},{2,0},{3,1},{4,6},{5,7},{6,4},{7,5},{8,10},{9,11},{10,... | collective-permute-start | bytes 589832 | tf_op jit(solution)/shard_map/ppermute | solution.py:401
  71.5 9.3 %collective-permute-start.17 = (bf16[2,192,128]{2,1,0:T(8,128)(2,1)S(1)}, bf16[2,192,128]{2,1,0:T(8,128)(2,1)S(1)}, u32[]{:S(2)}, u32[]{:S(2)}) collective-permute-start(bf16[2,192,128]{2,1,0:T(8,128)(2,1)S(1)} %get-tuple-element.42), channel_id=1, source_target_pairs={{0,2},{1,3},{2,0},{3,1},{4,6},{5,7},{6,4},{7,5},{8,10},{9,11},{10,... | collective-permute-start | bytes 294920 | tf_op jit(solution)/shard_map/ppermute | solution.py:401
  74.8 14.0 %collective-permute-start.28 = (bf16[192,512]{1,0:T(8,128)(2,1)S(1)}, bf16[192,512]{1,0:T(8,128)(2,1)S(1)}, u32[]{:S(2)}, u32[]{:S(2)}) collective-permute-start(bf16[192,512]{1,0:T(8,128)(2,1)S(1)} %get-tuple-element.45.refs_0_), channel_id=1, source_target_pairs={{0,4},{1,5},{2,6},{3,7},{4,0},{5,1},{6,2},{7,3},{8,12},{9,13},{10,... | collective-permute-start | bytes 589832 | tf_op jit(solution)/shard_map/ppermute | solution.py:401
  75.3 13.7 %collective-permute-start.29 = (bf16[192,512]{1,0:T(8,128)(2,1)S(1)}, bf16[192,512]{1,0:T(8,128)(2,1)S(1)}, u32[]{:S(2)}, u32[]{:S(2)}) collective-permute-start(bf16[192,512]{1,0:T(8,128)(2,1)S(1)} %get-tuple-element.45.refs_0_), channel_id=1, source_target_pairs={{0,6},{1,7},{2,4},{3,5},{4,2},{5,3},{6,0},{7,1},{8,14},{9,15},{10,... | collective-permute-start | bytes 589832 | tf_op jit(solution)/shard_map/ppermute | solution.py:401
  77.5 1.9 %collective-permute-start.24 = (s32[1,1]{1,0:T(1,128)}, s32[1,1]{1,0:T(1,128)}, u32[]{:S(2)}, u32[]{:S(2)}) collective-permute-start(s32[1,1]{1,0:T(1,128)} %param.14), channel_id=1, source_target_pairs={{0,1},{1,0},{2,3},{3,2},{4,5},{5,4},{6,7},{7,6},{8,9},{9,8},{10,11... | collective-permute-start | bytes 20 | tf_op jit(solution)/shard_map/ppermute | solution.py:401
  79.4 9.0 %collective-permute-start.18 = (bf16[2,192,128]{2,1,0:T(8,128)(2,1)S(1)}, bf16[2,192,128]{2,1,0:T(8,128)(2,1)S(1)}, u32[]{:S(2)}, u32[]{:S(2)}) collective-permute-start(bf16[2,192,128]{2,1,0:T(8,128)(2,1)S(1)} %get-tuple-element.43), channel_id=1, source_target_pairs={{0,4},{1,5},{2,6},{3,7},{4,0},{5,1},{6,2},{7,3},{8,12},{9,13},{10,... | collective-permute-start | bytes 294920 | tf_op jit(solution)/shard_map/ppermute | solution.py:401
  80.8 7.6 %collective-permute-start.19 = (bf16[2,192,128]{2,1,0:T(8,128)(2,1)S(1)}, bf16[2,192,128]{2,1,0:T(8,128)(2,1)S(1)}, u32[]{:S(2)}, u32[]{:S(2)}) collective-permute-start(bf16[2,192,128]{2,1,0:T(8,128)(2,1)S(1)} %get-tuple-element.44), channel_id=1, source_target_pairs={{0,6},{1,7},{2,4},{3,5},{4,2},{5,3},{6,0},{7,1},{8,14},{9,15},{10,... | collective-permute-start | bytes 294920 | tf_op jit(solution)/shard_map/ppermute | solution.py:401
  82.6 16.1 %collective-permute-start.39 = (bf16[2,768,128]{2,1,0:T(8,128)(2,1)S(1)}, bf16[2,768,128]{2,1,0:T(8,128)(2,1)S(1)}, u32[]{:S(2)}, u32[]{:S(2)}) collective-permute-start(bf16[2,768,128]{2,1,0:T(8,128)(2,1)S(1)} %get-tuple-element.70), channel_id=1, source_target_pairs={{0,1},{1,0},{2,3},{3,2},{4,5},{5,4},{6,7},{7,6},{8,9},{9,8},{10,11... | collective-permute-start | bytes 1179656 | tf_op jit(solution)/shard_map/ppermute | solution.py:401
  88.4 4.9 %collective-permute-start.20 = (bf16[2,192,128]{2,1,0:T(8,128)(2,1)S(1)}, bf16[2,192,128]{2,1,0:T(8,128)(2,1)S(1)}, u32[]{:S(2)}, u32[]{:S(2)}) collective-permute-start(bf16[2,192,128]{2,1,0:T(8,128)(2,1)S(1)} %get-tuple-element.41.refs_0_), channel_id=1, source_target_pairs={{0,1},{1,0},{2,3},{3,2},{4,5},{5,4},{6,7},{7,6},{8,9},{9,8},{10,11... | collective-permute-start | bytes 294920 | tf_op jit(solution)/shard_map/ppermute | solution.py:401
  88.4 4.9 %collective-permute-start.21 = (bf16[2,192,128]{2,1,0:T(8,128)(2,1)S(1)}, bf16[2,192,128]{2,1,0:T(8,128)(2,1)S(1)}, u32[]{:S(2)}, u32[]{:S(2)}) collective-permute-start(bf16[2,192,128]{2,1,0:T(8,128)(2,1)S(1)} %collective-permute-done.17.refs_1_), channel_id=1, source_target_pairs={{0,1},{1,0},{2,3},{3,2},{4,5},{5,4},{6,7},{7,6},{8,9},{9,8},{10,11... | collective-permute-start | bytes 294920 | tf_op jit(solution)/shard_map/ppermute | solution.py:401
  88.9 4.4 %collective-permute-start.22 = (bf16[2,192,128]{2,1,0:T(8,128)(2,1)S(1)}, bf16[2,192,128]{2,1,0:T(8,128)(2,1)S(1)}, u32[]{:S(2)}, u32[]{:S(2)}) collective-permute-start(bf16[2,192,128]{2,1,0:T(8,128)(2,1)S(1)} %collective-permute-done.18.refs_2_), channel_id=1, source_target_pairs={{0,1},{1,0},{2,3},{3,2},{4,5},{5,4},{6,7},{7,6},{8,9},{9,8},{10,11... | collective-permute-start | bytes 294920 | tf_op jit(solution)/shard_map/ppermute | solution.py:401
  89.0 4.3 %collective-permute-start.23 = (bf16[2,192,128]{2,1,0:T(8,128)(2,1)S(1)}, bf16[2,192,128]{2,1,0:T(8,128)(2,1)S(1)}, u32[]{:S(2)}, u32[]{:S(2)}) collective-permute-start(bf16[2,192,128]{2,1,0:T(8,128)(2,1)S(1)} %collective-permute-done.19.refs_3_), channel_id=1, source_target_pairs={{0,1},{1,0},{2,3},{3,2},{4,5},{5,4},{6,7},{7,6},{8,9},{9,8},{10,11... | collective-permute-start | bytes 294920 | tf_op jit(solution)/shard_map/ppermute | solution.py:401
  95.1 8.0 %collective-permute-start.30 = (bf16[800,128]{1,0:T(8,128)(2,1)S(1)}, bf16[800,128]{1,0:T(8,128)(2,1)S(1)}, u32[]{:S(2)}, u32[]{:S(2)}) collective-permute-start(bf16[800,128]{1,0:T(8,128)(2,1)S(1)} %get-tuple-element.57), channel_id=1, source_target_pairs={{0,2},{1,3},{2,0},{3,1},{4,6},{5,7},{6,4},{7,5},{8,10},{9,11},{10,... | collective-permute-start | bytes 614408 | tf_op jit(solution)/shard_map/ppermute | solution.py:401
  95.1 11.5 %collective-permute-start.31 = (bf16[800,128]{1,0:T(8,128)(2,1)S(1)}, bf16[800,128]{1,0:T(8,128)(2,1)S(1)}, u32[]{:S(2)}, u32[]{:S(2)}) collective-permute-start(bf16[800,128]{1,0:T(8,128)(2,1)S(1)} %get-tuple-element.58), channel_id=1, source_target_pairs={{0,4},{1,5},{2,6},{3,7},{4,0},{5,1},{6,2},{7,3},{8,12},{9,13},{10,... | collective-permute-start | bytes 614408 | tf_op jit(solution)/shard_map/ppermute | solution.py:401
  97.1 9.5 %collective-permute-start.32 = (bf16[800,128]{1,0:T(8,128)(2,1)S(1)}, bf16[800,128]{1,0:T(8,128)(2,1)S(1)}, u32[]{:S(2)}, u32[]{:S(2)}) collective-permute-start(bf16[800,128]{1,0:T(8,128)(2,1)S(1)} %get-tuple-element.59), channel_id=1, source_target_pairs={{0,6},{1,7},{2,4},{3,5},{4,2},{5,3},{6,0},{7,1},{8,14},{9,15},{10,... | collective-permute-start | bytes 614408 | tf_op jit(solution)/shard_map/ppermute | solution.py:401

commit v2 on v1

--- a/solution.py
+++ b/solution.py
@@ -55,6 +55,8 @@
 
 
 def part(index, size):
+    if isinstance(index, int):
+        return slice(index * size, (index + 1) * size)
     return pl.ds(pl.multiple_of(index * size, size), size)
 
 
@@ -85,7 +87,7 @@
     wkv_out[...] = jnp.concatenate(got[1:], axis=0).astype(jnp.bfloat16)
 
 
-def target_kernel(owners, most, assign_ref, tgt_ref):
+def target_kernel(owners, assign_ref, tgt_ref):
     groups = assign_ref.shape[1]
     owner = assign_ref[...]
     ids = lax.broadcasted_iota(jnp.int32, (max(owners, 8), groups), 0)
@@ -105,10 +107,7 @@
         ),
         axis=0,
     )
-    both = jnp.dot(both, mine, preferred_element_type=jnp.float32).astype(jnp.int32)
-    inner = jnp.bitwise_and(lax.broadcasted_iota(jnp.int32, tgt_ref.shape, 1), APP - 1)
-    source = both[0:8] * (owners // 2) + chip(0)
-    tgt_ref[...] = source * (most * APP) + both[8:16] * APP + inner
+    tgt_ref[...] = jnp.dot(both, mine, preferred_element_type=jnp.float32).astype(jnp.bfloat16)
 
 
 def stage_kernel(k0_ref, v0_ref, k1_ref, v1_ref, kk_ref, vt_ref, v_scr, sems):
@@ -141,14 +140,27 @@
     out_ref[...] = scr[...].astype(jnp.bfloat16)
 
 
-def project_q_kernel(chips, *refs):
-    x_refs, (w_ref, q_ref, x_ref) = refs[:chips], refs[chips:]
+def project_q_kernel(chips, w_ref, tgt_ref, *refs):
+    x_refs, (q_ref, x_ref) = refs[:chips], refs[chips:]
+    wide = w_ref.shape[0]
     rows = x_refs[0].shape[0]
     for s in range(chips):
         x_ref[part(chip(s), rows), :] = x_refs[s][...]
-    q_ref[...] = lax.dot_general(
+    q_ref[wide:, :] = jnp.zeros_like(q_ref[wide:, :])
+    q_ref[wide:, 0:rows] = tgt_ref[...]
+    q_ref[0:wide, :] = lax.dot_general(
         w_ref[...], x_ref[...], NT, preferred_element_type=jnp.float32
     ).astype(jnp.bfloat16)
+
+
+def slots_of(names, chips, most, source):
+    both = names.astype(jnp.float32).astype(jnp.int32)
+    inner = jnp.bitwise_and(lax.broadcasted_iota(jnp.int32, both[0:8].shape, 1), APP - 1)
+    return (both[0:8] * chips + source) * (most * APP) + both[8:16] * APP + inner
+
+
+def own_kernel(chips, most, tgt_ref, out_ref):
+    out_ref[...] = slots_of(tgt_ref[...], chips, most, chip(0))
 
 
 def project_kv_kernel(chips, x_ref, w_ref, kv_ref, *out_refs):
@@ -162,15 +174,18 @@
         out_refs[s][1] = kv_ref[wide:, part(chip(s), rows)]
 
 
-def hits_kernel(chips, *refs):
-    t_refs, refs = refs[:chips], refs[chips:]
+def hits_kernel(chips, most, own_ref, *refs):
+    q_refs, refs = refs[: chips - 1], refs[chips - 1 :]
     out_refs, (t_scr,) = refs[:chips], refs[chips:]
-    rows = t_refs[0].shape[1]
-    for s in range(chips):
-        t_scr[:, part(chip(s), rows)] = t_refs[s][...]
+    slots, tokens = out_refs[0].shape
+    rows = tokens // chips
+    t_scr[:, part(chip(0), rows)] = own_ref[...]
+    for s in range(1, chips):
+        q_ref = q_refs[s - 1]
+        names = q_ref[q_ref.shape[0] - 16 :, 0:rows]
+        t_scr[:, part(chip(s), rows)] = slots_of(names, chips, most, chip(s))
     targets = t_scr[0:1, :]
-    slots = out_refs[0].shape[0]
-    slot = lax.broadcasted_iota(jnp.int32, (slots, chips * rows), 0)
+    slot = lax.broadcasted_iota(jnp.int32, (slots, tokens), 0)
     for s in range(chips):
         hit = slot == targets - chip(s) * slots
         out_refs[s][...] = hit.astype(jnp.float32).astype(jnp.bfloat16)
@@ -206,21 +221,42 @@
     return jnp.concatenate((value, jnp.ones((16, value.shape[1]), value.dtype)), axis=0)
 
 
-def cached_kernel(chips, flip, tile, len0_ref, len1_ref, *refs):
-    q_refs, refs = refs[: chips // 2], refs[chips // 2 :]
-    kk_ref, vt_ref, q_all, acc_ref, top_ref, total_ref = refs
-    wide = q_refs[0].shape[0]
-    for i in range(chips // 2):
-        at = jnp.bitwise_and(chip(i), chips // 2 - 1)
-        q_all[part(at, wide), :] = q_refs[i][...]
+def odd_chip():
+    return jnp.bitwise_and(chip(0), 1)
+
+
+def heads_of(chips, kind):
+    half = HEADS // 2
+    if kind < 2:
+        return head_group(chips, kind), half
+    if kind == 2:
+        return head_group(chips, 0) + odd_chip() * (half - 1), 1
+    return head_group(chips, 0) + (1 - odd_chip()), half - 1
+
+
+def cached_kernel(chips, kind, tile, len0_ref, len1_ref, *refs):
+    used = 1 if kind == 2 else chips // 2
+    q_refs, refs = refs[:used], refs[used:]
+    kk_ref, vt_ref, q_all, acc_ref, top_ref, total_ref = refs[:6]
+    wide = q_refs[0].shape[0] - 16
+    first, count = heads_of(chips, kind)
+    if kind == 2:
+        q_all[...] = q_refs[0][pl.ds(pl.multiple_of(odd_chip() * (wide - HD), wide - HD), HD), :]
+    else:
+        q_scr = q_all if kind < 2 else refs[6]
+        for i in range(used):
+            at = jnp.bitwise_and(chip(i), chips // 2 - 1)
+            q_scr[part(at, wide), :] = q_refs[i][0:wide, :]
+        if kind == 3:
+            rest = pl.ds(pl.multiple_of((1 - odd_chip()) * HD, HD), count * HD)
+            q_all[...] = q_scr[rest, :]
     tokens = q_all.shape[1]
     capacity = kk_ref.shape[1]
     short = min(2 * BLOCK, capacity)
-    first = head_group(chips, flip)
     lengths = (len0_ref[0], len1_ref[0])
 
     def run(sizes):
-        def head(h, carry):
+        def head(h):
             at = part(h, HD)
             row = part(h, 8)
             keys = [kk_ref[i, 0 : sizes[i], part(first + h, HD)] for i in range(2)]
@@ -261,9 +297,11 @@
 
             step = min(2 * tile, tokens)
             each_tile(tokens // step, step, several)
-            return carry
-
-        lax.fori_loop(0, HEADS // 2, head, 0)
+
+        if count == 1:
+            head(0)
+        else:
+            lax.fori_loop(0, count, lambda h, c: (head(h), c)[1], 0)
 
     brief = [length * BLOCK <= short for length in lengths]
     if capacity <= short:
@@ -283,31 +321,39 @@
     return stat[0:8] + stat[8:16] + stat[16:24]
 
 
-def appended_kernel(chips, tile, *refs):
-    kv_refs, refs = refs[: 2 * chips], refs[2 * chips :]
-    states, refs = (refs[0:4], refs[4:8]), refs[8:]
+def dense_join_kernel(chips, *refs):
+    kv_refs, out_ref = refs[:chips], refs[chips]
+    for s in range(chips):
+        for i in range(2):
+            out_ref[i, part(chip(s), kv_refs[s].shape[1]), :] = kv_refs[s][i]
+
+
+def appended_kernel(chips, kinds, tile, *refs):
+    kv_refs, refs = refs[:2], refs[2:]
+    states = [refs[4 * i : 4 * i + 4] for i in range(len(kinds))]
+    refs = refs[4 * len(kinds) :]
     out_refs, (kt_scr, vt_scr, out_scr, level_scr) = refs[:chips], refs[chips:]
-    wide, rows = kv_refs[0].shape[1], kv_refs[0].shape[2]
+    rows = kv_refs[0].shape[2]
     for j in range(2):
-        for s in range(chips):
-            kt_scr[part(chip(s), wide), j * rows : (j + 1) * rows] = kv_refs[j * chips + s][0]
-            vt_scr[part(chip(s), wide), j * rows : (j + 1) * rows] = kv_refs[j * chips + s][1]
+        kt_scr[:, j * rows : (j + 1) * rows] = kv_refs[j][0]
+        vt_scr[:, j * rows : (j + 1) * rows] = kv_refs[j][1]
     tokens = level_scr.shape[1]
 
     def several(j):
         lanes = pl.ds(j, tile)
-        units = [(flip, h) for flip in range(2) for h in range(HEADS // 2)]
-        heads = [head_group(chips, flip) + h for flip, h in units]
+        groups = [heads_of(chips, kind) for kind in kinds]
+        units = [(i, h) for i, (_, count) in enumerate(groups) for h in range(count)]
+        heads = [groups[i][0] + h for i, h in units]
         scores = [
             lax.dot_general(
                 kt_scr[part(head, HD), :],
-                states[flip][0][h * HD : (h + 1) * HD, lanes],
+                states[i][0][h * HD : (h + 1) * HD, lanes],
                 TN,
                 preferred_element_type=jnp.float32,
             )
-            for (flip, h), head in zip(units, heads)
+            for (i, h), head in zip(units, heads)
         ]
-        olds = [states[flip][2][8 * h : 8 * h + 1, lanes] for flip, h in units]
+        olds = [states[i][2][8 * h : 8 * h + 1, lanes] for i, h in units]
         tops = [jnp.maximum(jnp.max(s, axis=0, keepdims=True), o) for s, o in zip(scores, olds)]
         weights = [
             jnp.exp2((s - top) * EXP_SCALE).astype(jnp.bfloat16) for s, top in zip(scores, tops)
@@ -318,11 +364,11 @@
         ]
         row = lax.broadcasted_iota(jnp.int32, (8, tile), 0)
         levels = jnp.zeros((8, tile), jnp.float32)
-        for (flip, h), head, old_top, top, numer in zip(units, heads, olds, tops, numers):
+        for (i, h), head, old_top, top, numer in zip(units, heads, olds, tops, numers):
             old = jnp.exp2((old_top - top) * EXP_SCALE)
-            total = numer[HD : HD + 1] + states[flip][3][8 * h : 8 * h + 1, lanes] * old
+            total = numer[HD : HD + 1] + states[i][3][8 * h : 8 * h + 1, lanes] * old
             inverse = 1.0 / total
-            mixed = states[flip][1][h * HD : (h + 1) * HD, lanes] * (old * inverse)
+            mixed = states[i][1][h * HD : (h + 1) * HD, lanes] * (old * inverse)
             mixed = mixed + numer[:HD] * inverse
             out_scr[part(head, HD), lanes] = mixed.astype(jnp.bfloat16)
             levels = jnp.where(row == head, top * EXP_SCALE + jnp.log2(total), levels)
@@ -378,6 +424,11 @@
         out_ref[:, lo:hi] = mixed.T.astype(jnp.bfloat16)
 
 
+def cached_kinds(owners):
+    whole_head = owners // 2 == 4 and 4 * HD * 3 == 2 * WIDTH
+    return (2, 3, 1) if whole_head else (0, 1)
+
+
 def body(tokens, query_weight, key_weight, value_weight, cache_keys, cache_values, lengths, assign):
     owners = lax.axis_size("patch")
     shards = lax.axis_size("stream")
@@ -427,12 +478,11 @@
     other_values = twin(cache_values[0])
     other_length = twin(lengths)
     tgt = call(
-        functools.partial(target_kernel, owners, most),
-        shape(8, rows, dtype=jnp.int32),
+        functools.partial(target_kernel, owners),
+        shape(16, rows),
         (assign.reshape(1, groups),),
         flops=1 << 20,
     )
-    t_all = far([tgt] * chips)
     kk, vt = call(
         stage_kernel,
         (shape(2, cached_rows, WIDTH), shape(2, WIDTH, cached_rows)),
@@ -456,12 +506,18 @@
     wq_full = whole(wq_all, 1)
     q_own, x_full = call(
         functools.partial(project_q_kernel, chips),
-        (shape(wide, half), shape(half, features)),
-        (*x_all, wq_full),
+        (shape(wide + 16, half), shape(half, features)),
+        (wq_full, tgt, *x_all),
         flops=2 * wide * half * features,
     )
     near = list(range(1, chips // 2)) + list(range(chips // 2, chips))
     q_all = far([q_own] * chips, order=near)
+    own = call(
+        functools.partial(own_kernel, chips, most),
+        shape(8, rows, dtype=jnp.int32),
+        (tgt,),
+        flops=1 << 20,
+    )
     wkv_full = whole(wkv_all, 2)
     projected = call(
         functools.partial(project_kv_kernel, chips),
@@ -470,11 +526,14 @@
         flops=4 * wide * half * features,
     )
     kv_own, dense = projected[0], far(projected[1:])
-    dense = dense + [twin(d) for d in dense]
+    dense = call(
+        functools.partial(dense_join_kernel, chips), shape(2, WIDTH, rows), dense, flops=1 << 20
+    )
+    other_dense = twin(dense)
     hits = call(
-        functools.partial(hits_kernel, chips),
+        functools.partial(hits_kernel, chips, most),
         (shape(2 * slots, half),) * chips,
-        t_all,
+        (own, *q_all[1:]),
         scratch=[pltpu.VMEM((8, half), jnp.int32)],
         flops=1 << 20,
     )
@@ -487,26 +546,29 @@
     sent = far(selected)
     tile = min(256, half)
 
-    def cached(flip):
-        first = flip * (chips // 2)
+    def cached(kind, count):
+        pieces = (q_all[: chips // 2], q_all[chips // 2 :], q_all[:1], q_all[: chips // 2])[kind]
         return call(
-            functools.partial(cached_kernel, chips, flip, tile),
+            functools.partial(cached_kernel, chips, kind, tile),
             (
-                shape(WIDTH // 2, half),
-                shape(WIDTH // 2, half, dtype=f32),
-                shape(4 * HEADS, half, dtype=f32),
-                shape(4 * HEADS, half, dtype=f32),
+                shape(count * HD, half),
+                shape(count * HD, half, dtype=f32),
+                shape(8 * count, half, dtype=f32),
+                shape(8 * count, half, dtype=f32),
             ),
-            (lengths[0], other_length[0], *q_all[first : first + chips // 2], kk, vt),
+            (lengths[0], other_length[0], *pieces, kk, vt),
             smem=2,
-            flops=4 * cached_rows * half * WIDTH,
+            scratch=[pltpu.VMEM((WIDTH // 2, half), bf16)] if kind == 3 else [],
+            flops=8 * cached_rows * half * count * HD,
         )
 
-    states = [*cached(0), *cached(1)]
+    kinds = cached_kinds(owners)
+    counts = {0: HEADS // 2, 1: HEADS // 2, 2: 1, 3: HEADS // 2 - 1}
+    states = [array for kind in kinds for array in cached(kind, counts[kind])]
     parts = call(
-        functools.partial(appended_kernel, chips, min(512, half)),
+        functools.partial(appended_kernel, chips, kinds, min(512, half)),
         (shape(WIDTH + STAT_ROWS, rows),) * chips,
-        (*dense, *states),
+        (dense, other_dense, *states),
         scratch=[
             pltpu.VMEM((WIDTH, 2 * rows), bf16),
             pltpu.VMEM((WIDTH, 2 * rows), bf16),

time: 108 us -> 107 us (level)
  starting transfers between devices: 37.2 us -> 29.4 us
  waiting for transfers between devices: 48.7 us -> 53.9 us
    ppermute x40 -> x34, starting transfers between devices: 37.2 us -> 29.4 us  [swap(): return lax.ppermute(x, axis, [(i, i ^ r) for i in range(size)])]
    ppermute x40 -> x34, waiting for transfers between devices: 48.7 us -> 53.9 us  [swap(): return lax.ppermute(x, axis, [(i, i ^ r) for i in range(size)])]
    pallas_call x16 -> x19, Pallas kernels: 19.3 us -> 19.9 us  [call(): pl.pallas_call(kernel, out_shape=out_shape, in_specs=[SMEM] * smem + [VME...]
  transfers between devices with their start and end apart: 40 -> 34, of which waited for: 14 -> 14; matrix products, arithmetic and copies ran while one was open for 0% -> 0% of each run, Pallas kernels for 15% -> 16%
where the time goes in v2:
time: 107 us; the launch traced here: 106 us
  waiting for transfers between devices  53.9 us (50%)
  starting transfers between devices  29.4 us (27%)
  Pallas kernels  19.9 us (19%)
  between operations  1.52 us (1%)
    ppermute x34, waiting for transfers between devices, swap(): return lax.ppermute(x, axis, [(i, i ^ r) for i in range(size)])  53.9 us
    ppermute x34, starting transfers between devices, swap(): return lax.ppermute(x, axis, [(i, i ^ r) for i in range(size)])  29.4 us
    pallas_call x19, Pallas kernels, call(): pl.pallas_call(kernel, out_shape=out_shape, in_specs=[SMEM] * smem + [VME...  19.9 us
  transfers between devices with their start and end apart: 34, of which 14 were waited for; matrix products, arithmetic and copies ran while one was open for 0% of the time, Pallas kernels for 16%

profile of v2, /device:TPU:0, one launch (start us, length us, event | category | flops | bytes accessed | tf_op | source)
XLA Modules:
  0.0 105.7 jit_solution(3506630866442043593)
XLA Ops:
  0.7 2.4 %shard_map.103 = (bf16[96,384]{1,0:T(8,128)(2,1)}, bf16[192,384]{1,0:T(8,128)(2,1)}) custom-call(bf16[384,768]{1,0:T(8,128)(2,1)} %wq_ref.1, bf16[384,768]{1,0:T(8,128)(2,1)} %wk_ref.1, bf16[384,768]{1,0:T(8,128)(2,1)} %wv_ref.1), custom_call_target="tpu_custom_call" | custom-call | flops 169869312 | bytes 1048576 | tf_op jit(solution)/shard_map/pallas_call | solution.py:34
  3.0 3.1 %collective-permute-start = (bf16[96,384]{1,0:T(8,128)(2,1)}, bf16[96,384]{1,0:T(8,128)(2,1)S(1)}, u32[]{:S(2)}, u32[]{:S(2)}) collective-permute-start(bf16[96,384]{1,0:T(8,128)(2,1)} %get-tuple-element.42.refs_0_), channel_id=1, source_target_pairs={{0,8},{8,0},{16,24},{24,16},{1,9},{9,1},{17,25},{25,17},{2,10},{10... | collective-permute-start | bytes 221192 | tf_op jit(solution)/shard_map/ppermute | solution.py:452
  6.1 2.6 %collective-permute-start.1 = (bf16[96,384]{1,0:T(8,128)(2,1)}, bf16[96,384]{1,0:T(8,128)(2,1)S(1)}, u32[]{:S(2)}, u32[]{:S(2)}) collective-permute-start(bf16[96,384]{1,0:T(8,128)(2,1)} %get-tuple-element.42.refs_0_), channel_id=1, source_target_pairs={{0,16},{8,24},{16,0},{24,8},{1,17},{9,25},{17,1},{25,9},{2,18},{10... | collective-permute-start | bytes 221192 | tf_op jit(solution)/shard_map/ppermute | solution.py:452
  8.7 0.0 collective-permute-start.2
  8.7 0.0 collective-permute-start.3
  8.7 0.0 collective-permute-done.refs_1_
  8.7 0.5 collective-permute-start.4
  9.3 4.9 %collective-permute-done.1.refs_2_ = bf16[96,384]{1,0:T(8,128)(2,1)S(1)} collective-permute-done((bf16[96,384]{1,0:T(8,128)(2,1)}, bf16[96,384]{1,0:T(8,128)(2,1)S(1)}, u32[]{:S(2)}, u32[]{:S(2)}) %collective-permute-start.1) | collective-permute-done | bytes 73760 | tf_op jit(solution)/shard_map/ppermute | solution.py:452
  14.2 0.5 collective-permute-start.10
  14.7 0.5 collective-permute-done.2.refs_3_
  15.2 2.8 %collective-permute-start.11 = (bf16[192,384]{1,0:T(8,128)(2,1)}, bf16[192,384]{1,0:T(8,128)(2,1)S(1)}, u32[]{:S(2)}, u32[]{:S(2)}) collective-permute-start(bf16[192,384]{1,0:T(8,128)(2,1)} %get-tuple-element.44.refs_0_), channel_id=1, source_target_pairs={{0,16},{8,24},{16,0},{24,8},{1,17},{9,25},{17,1},{25,9},{2,18},{10... | collective-permute-start | bytes 442376 | tf_op jit(solution)/shard_map/ppermute | solution.py:452
  18.0 0.7 collective-permute-start.12
  18.7 0.0 collective-permute-start.13
  18.7 0.5 collective-permute-start.6
  19.2 1.2 %collective-permute-done.6.refs_7_ = bf16[96,384]{1,0:T(8,128)(2,1)S(1)} collective-permute-done((bf16[96,384]{1,0:T(8,128)(2,1)S(1)}, bf16[96,384]{1,0:T(8,128)(2,1)S(1)}, u32[]{:S(2)}, u32[]{:S(2)}) %collective-permute-start.6) | collective-permute-done | bytes 73760 | tf_op jit(solution)/shard_map/ppermute | solution.py:452
  20.4 0.1 collective-permute-start.22
  20.5 2.9 %collective-permute-done.10.refs_1_ = bf16[192,384]{1,0:T(8,128)(2,1)S(1)} collective-permute-done((bf16[192,384]{1,0:T(8,128)(2,1)}, bf16[192,384]{1,0:T(8,128)(2,1)S(1)}, u32[]{:S(2)}, u32[]{:S(2)}) %collective-permute-start.10) | collective-permute-done | bytes 147488 | tf_op jit(solution)/shard_map/ppermute | solution.py:452
  23.4 0.2 shard_map.106.refs_0_
  23.6 5.8 %collective-permute-done.11.refs_2_ = bf16[192,384]{1,0:T(8,128)(2,1)S(1)} collective-permute-done((bf16[192,384]{1,0:T(8,128)(2,1)}, bf16[192,384]{1,0:T(8,128)(2,1)S(1)}, u32[]{:S(2)}, u32[]{:S(2)}) %collective-permute-start.11) | collective-permute-done | bytes 147488 | tf_op jit(solution)/shard_map/ppermute | solution.py:452
  29.4 1.5 %collective-permute-start.7 = (bf16[128,1536]{1,0:T(8,128)(2,1)S(1)}, bf16[128,1536]{1,0:T(8,128)(2,1)S(1)}, u32[]{:S(2)}, u32[]{:S(2)}) collective-permute-start(bf16[128,1536]{1,0:T(8,128)(2,1)S(1)} %shard_map.106.refs_0_), channel_id=1, source_target_pairs={{0,2},{1,3},{2,0},{3,1},{4,6},{5,7},{6,4},{7,5},{8,10},{9,11},{10,... | collective-permute-start | bytes 1179656 | tf_op jit(solution)/shard_map/ppermute | solution.py:452
  30.9 1.5 %collective-permute-start.8 = (bf16[128,1536]{1,0:T(8,128)(2,1)S(1)}, bf16[128,1536]{1,0:T(8,128)(2,1)S(1)}, u32[]{:S(2)}, u32[]{:S(2)}) collective-permute-start(bf16[128,1536]{1,0:T(8,128)(2,1)S(1)} %shard_map.106.refs_0_), channel_id=1, source_target_pairs={{0,4},{1,5},{2,6},{3,7},{4,0},{5,1},{6,2},{7,3},{8,12},{9,13},{10,... | collective-permute-start | bytes 1179656 | tf_op jit(solution)/shard_map/ppermute | solution.py:452
  32.4 0.5 collective-permute-start.9
  32.9 7.8 %collective-permute-done.7.refs_1_ = bf16[128,1536]{1,0:T(8,128)(2,1)S(1)} collective-permute-done((bf16[128,1536]{1,0:T(8,128)(2,1)S(1)}, bf16[128,1536]{1,0:T(8,128)(2,1)S(1)}, u32[]{:S(2)}, u32[]{:S(2)}) %collective-permute-start.7) | collective-permute-done | bytes 393248 | tf_op jit(solution)/shard_map/ppermute | solution.py:452
  40.6 7.2 %collective-permute-done.8.refs_2_ = bf16[128,1536]{1,0:T(8,128)(2,1)S(1)} collective-permute-done((bf16[128,1536]{1,0:T(8,128)(2,1)S(1)}, bf16[128,1536]{1,0:T(8,128)(2,1)S(1)}, u32[]{:S(2)}, u32[]{:S(2)}) %collective-permute-start.8) | collective-permute-done | bytes 393248 | tf_op jit(solution)/shard_map/ppermute | solution.py:452
  47.9 0.5 collective-permute-start.16
  48.4 0.2 shard_map.105.tgt_ref
  48.6 0.9 copy-done.4
  49.5 0.1 shard_map.104.w_ref
  49.7 0.0 copy-start.3
  49.7 0.8 shard_map.107
  50.5 1.6 %collective-permute-start.24 = (bf16[208,512]{1,0:T(8,128)(2,1)S(1)}, bf16[208,512]{1,0:T(8,128)(2,1)S(1)}, u32[]{:S(2)}, u32[]{:S(2)}) collective-permute-start(bf16[208,512]{1,0:T(8,128)(2,1)S(1)} %get-tuple-element.49.refs_0_), channel_id=1, source_target_pairs={{0,2},{1,3},{2,0},{3,1},{4,6},{5,7},{6,4},{7,5},{8,10},{9,11},{10,... | collective-permute-start | bytes 638984 | tf_op jit(solution)/shard_map/ppermute | solution.py:452
  52.0 1.5 %collective-permute-start.25 = (bf16[208,512]{1,0:T(8,128)(2,1)S(1)}, bf16[208,512]{1,0:T(8,128)(2,1)S(1)}, u32[]{:S(2)}, u32[]{:S(2)}) collective-permute-start(bf16[208,512]{1,0:T(8,128)(2,1)S(1)} %get-tuple-element.49.refs_0_), channel_id=1, source_target_pairs={{0,4},{1,5},{2,6},{3,7},{4,0},{5,1},{6,2},{7,3},{8,12},{9,13},{10,... | collective-permute-start | bytes 638984 | tf_op jit(solution)/shard_map/ppermute | solution.py:452
  53.6 0.5 collective-permute-start.26
  54.1 0.3 shard_map.108.w_ref
  54.4 0.9 shard_map.109
  55.3 3.4 %collective-permute-done.24.refs_1_.refs_0_ = bf16[208,512]{1,0:T(8,128)(2,1)S(1)} collective-permute-done((bf16[208,512]{1,0:T(8,128)(2,1)S(1)}, bf16[208,512]{1,0:T(8,128)(2,1)S(1)}, u32[]{:S(2)}, u32[]{:S(2)}) %collective-permute-start.24) | collective-permute-done | bytes 213024 | tf_op jit(solution)/shard_map/ppermute | solution.py:452
  58.7 1.5 %collective-permute-start.17 = (bf16[2,192,128]{2,1,0:T(8,128)(2,1)S(1)}, bf16[2,192,128]{2,1,0:T(8,128)(2,1)S(1)}, u32[]{:S(2)}, u32[]{:S(2)}) collective-permute-start(bf16[2,192,128]{2,1,0:T(8,128)(2,1)S(1)} %get-tuple-element.46), channel_id=1, source_target_pairs={{0,2},{1,3},{2,0},{3,1},{4,6},{5,7},{6,4},{7,5},{8,10},{9,11},{10,... | collective-permute-start | bytes 294920 | tf_op jit(solution)/shard_map/ppermute | solution.py:452
  60.2 2.6 %collective-permute-done.25.refs_0_.refs_1_ = bf16[208,512]{1,0:T(8,128)(2,1)S(1)} collective-permute-done((bf16[208,512]{1,0:T(8,128)(2,1)S(1)}, bf16[208,512]{1,0:T(8,128)(2,1)S(1)}, u32[]{:S(2)}, u32[]{:S(2)}) %collective-permute-start.25) | collective-permute-done | bytes 213024 | tf_op jit(solution)/shard_map/ppermute | solution.py:452
  62.7 1.5 %collective-permute-done.26.refs_1_.refs_2_ = bf16[208,512]{1,0:T(8,128)(2,1)S(1)} collective-permute-done((bf16[208,512]{1,0:T(8,128)(2,1)S(1)}, bf16[208,512]{1,0:T(8,128)(2,1)S(1)}, u32[]{:S(2)}, u32[]{:S(2)}) %collective-permute-start.26) | collective-permute-done | bytes 213024 | tf_op jit(solution)/shard_map/ppermute | solution.py:452
  64.2 0.4 shard_map.118
  64.7 0.0 copy-start.1
  64.7 0.6 shard_map.119
  65.3 1.5 %collective-permute-start.30 = (bf16[2,192,256]{2,1,0:T(8,128)(2,1)S(1)}, bf16[2,192,256]{2,1,0:T(8,128)(2,1)S(1)}, u32[]{:S(2)}, u32[]{:S(2)}) collective-permute-start(bf16[2,192,256]{2,1,0:T(8,128)(2,1)S(1)} %get-tuple-element.74), channel_id=1, source_target_pairs={{0,2},{1,3},{2,0},{3,1},{4,6},{5,7},{6,4},{7,5},{8,10},{9,11},{10,... | collective-permute-start | bytes 589832 | tf_op jit(solution)/shard_map/ppermute | solution.py:452
  66.8 0.6 collective-permute-start.18
  67.4 1.5 %collective-permute-start.19 = (bf16[2,192,128]{2,1,0:T(8,128)(2,1)S(1)}, bf16[2,192,128]{2,1,0:T(8,128)(2,1)S(1)}, u32[]{:S(2)}, u32[]{:S(2)}) collective-permute-start(bf16[2,192,128]{2,1,0:T(8,128)(2,1)S(1)} %get-tuple-element.48), channel_id=1, source_target_pairs={{0,6},{1,7},{2,4},{3,5},{4,2},{5,3},{6,0},{7,1},{8,14},{9,15},{10,... | collective-permute-start | bytes 294920 | tf_op jit(solution)/shard_map/ppermute | solution.py:452
  68.9 4.3 %collective-permute-done.18.refs_2_ = bf16[2,192,128]{2,1,0:T(8,128)(2,1)S(1)} collective-permute-done((bf16[2,192,128]{2,1,0:T(8,128)(2,1)S(1)}, bf16[2,192,128]{2,1,0:T(8,128)(2,1)S(1)}, u32[]{:S(2)}, u32[]{:S(2)}) %collective-permute-start.18) | collective-permute-done | bytes 98336 | tf_op jit(solution)/shard_map/ppermute | solution.py:452
  73.1 0.1 collective-permute-start.31
  73.2 1.7 %collective-permute-start.32 = (bf16[2,192,256]{2,1,0:T(8,128)(2,1)S(1)}, bf16[2,192,256]{2,1,0:T(8,128)(2,1)S(1)}, u32[]{:S(2)}, u32[]{:S(2)}) collective-permute-start(bf16[2,192,256]{2,1,0:T(8,128)(2,1)S(1)} %get-tuple-element.76), channel_id=1, source_target_pairs={{0,6},{1,7},{2,4},{3,5},{4,2},{5,3},{6,0},{7,1},{8,14},{9,15},{10,... | collective-permute-start | bytes 589832 | tf_op jit(solution)/shard_map/ppermute | solution.py:452
  74.9 0.1 collective-permute-start.20
  75.7 5.2 %collective-permute-done.31.refs_2_ = bf16[2,192,256]{2,1,0:T(8,128)(2,1)S(1)} collective-permute-done((bf16[2,192,256]{2,1,0:T(8,128)(2,1)S(1)}, bf16[2,192,256]{2,1,0:T(8,128)(2,1)S(1)}, u32[]{:S(2)}, u32[]{:S(2)}) %collective-permute-start.31) | collective-permute-done | bytes 196640 | tf_op jit(solution)/shard_map/ppermute | solution.py:452
  80.9 0.1 shard_map.120
  81.0 0.6 collective-permute-start.33
  81.6 1.8 %shard_map.111 = (bf16[2,768,768]{2,1,0:T(8,128)(2,1)S(1)}, bf16[2,768,768]{2,1,0:T(8,128)(2,1)S(1)}) custom-call(bf16[768,768]{1,0:T(8,128)(2,1)S(1)} %bitcast.13, bf16[768,768]{1,0:T(8,128)(2,1)S(1)} %bitcast.15, bf16[768,768]{1,0:T(8,128)(2,1)S(1)} %collective-permute-done.22.k1_ref, bf16[768,768]{1,0:T(8,128)(2,1)S(1)} %collective-permute-done.23.v1_ref), custom_call_target="tpu_custom_call" | custom-call | flops 1048576 | bytes 1048576 | tf_op jit(solution)/shard_map/pallas_call | solution.py:34
  83.4 2.7 %shard_map.113 = (bf16[256,512]{1,0:T(8,128)(2,1)S(1)}, f32[256,512]{1,0:T(8,128)S(1)}, f32[16,512]{1,0:T(8,128)S(1)}, f32[16,512]{1,0:T(8,128)S(1)}) custom-call(s32[1]{0:T(128)} %bitcast.10.len0_ref, s32[1]{0:T(128)} %bitcast.3.len1_ref, bf16[208,512]{1,0:T(8,128)(2,1)S(1)} %get-tuple-element.49.refs_0_, ...), custom_call_target="tpu_custom_call" | custom-call | flops 805306368 | bytes 1048576 | tf_op jit(solution)/shard_map/pallas_call | solution.py:34
  86.1 1.9 %shard_map.112 = (bf16[128,512]{1,0:T(8,128)(2,1)S(1)}, f32[128,512]{1,0:T(8,128)S(1)}, f32[8,512]{1,0:T(8,128)S(1)}, f32[8,512]{1,0:T(8,128)S(1)}) custom-call(s32[1]{0:T(128)} %bitcast.9.len0_ref, s32[1]{0:T(128)} %bitcast.3.len1_ref, bf16[208,512]{1,0:T(8,128)(2,1)S(1)} %get-tuple-element.49.refs_0_, ...), custom_call_target="tpu_custom_call" | custom-call | flops 402653184 | bytes 1048576 | tf_op jit(solution)/shard_map/pallas_call | solution.py:34
  87.9 3.6 %shard_map.114 = (bf16[384,512]{1,0:T(8,128)(2,1)S(1)}, f32[384,512]{1,0:T(8,128)S(1)}, f32[24,512]{1,0:T(8,128)S(1)}, f32[24,512]{1,0:T(8,128)S(1)}) custom-call(s32[1]{0:T(128)} %bitcast.11.len0_ref, s32[1]{0:T(128)} %bitcast.3.len1_ref, bf16[208,512]{1,0:T(8,128)(2,1)S(1)} %collective-permute-done.25.refs_0_.refs_1_, ...), custom_call_target="tpu_custom_call" | custom-call | flops 1207959552 | bytes 1048576 | tf_op jit(solution)/shard_map/pallas_call | solution.py:34
  91.6 1.8 %shard_map.115 = (bf16[800,128]{1,0:T(8,128)(2,1)S(1)}, bf16[800,128]{1,0:T(8,128)(2,1)S(1)}, bf16[800,128]{1,0:T(8,128)(2,1)S(1)}, bf16[800,128]{1,0:T(8,128)(2,1)S(1)}) custom-call(bf16[2,768,128]{2,1,0:T(8,128)(2,1)S(1)} %shard_map.110.refs_0_, bf16[2,768,128]{2,1,0:T(8,128)(2,1)S(1)} %collective-permute-done.20.refs_1_, ...), custom_call_target="tpu_custom_call" | custom-call | flops 402653184 | bytes 1048576 | tf_op jit(solution)/shard_map/pallas_call | solution.py:34
  93.3 0.1 collective-permute-start.27
  93.4 1.7 %collective-permute-start.28 = (bf16[800,128]{1,0:T(8,128)(2,1)S(1)}, bf16[800,128]{1,0:T(8,128)(2,1)S(1)}, u32[]{:S(2)}, u32[]{:S(2)}) collective-permute-start(bf16[800,128]{1,0:T(8,128)(2,1)S(1)} %get-tuple-element.66), channel_id=1, source_target_pairs={{0,4},{1,5},{2,6},{3,7},{4,0},{5,1},{6,2},{7,3},{8,12},{9,13},{10,... | collective-permute-start | bytes 614408 | tf_op jit(solution)/shard_map/ppermute | solution.py:452
  95.2 1.7 %collective-permute-start.29 = (bf16[800,128]{1,0:T(8,128)(2,1)S(1)}, bf16[800,128]{1,0:T(8,128)(2,1)S(1)}, u32[]{:S(2)}, u32[]{:S(2)}) collective-permute-start(bf16[800,128]{1,0:T(8,128)(2,1)S(1)} %get-tuple-element.67), channel_id=1, source_target_pairs={{0,6},{1,7},{2,4},{3,5},{4,2},{5,3},{6,0},{7,1},{8,14},{9,15},{10,... | collective-permute-start | bytes 614408 | tf_op jit(solution)/shard_map/ppermute | solution.py:452
  96.9 1.2 %shard_map.121 = (bf16[256,768]{1,0:T(8,128)(2,1)}, bf16[256,768]{1,0:T(8,128)(2,1)}) custom-call(bf16[2,768,128]{2,1,0:T(8,128)(2,1)S(1)} %get-tuple-element.77.mine_ref, bf16[2,768,128]{2,1,0:T(8,128)(2,1)S(1)} %collective-permute-done.33.got_ref), custom_call_target="tpu_custom_call" | custom-call | flops 1048576 | bytes 1048576 | tf_op jit(solution)/shard_map/pallas_call | solution.py:34
  98.1 3.2 %collective-permute-done.27.refs_1_ = bf16[800,128]{1,0:T(8,128)(2,1)S(1)} collective-permute-done((bf16[800,128]{1,0:T(8,128)(2,1)S(1)}, bf16[800,128]{1,0:T(8,128)(2,1)S(1)}, u32[]{:S(2)}, u32[]{:S(2)}) %collective-permute-start.27) | collective-permute-done | bytes 204832 | tf_op jit(solution)/shard_map/ppermute | solution.py:452
  101.4 3.4 %collective-permute-done.28.refs_2_ = bf16[800,128]{1,0:T(8,128)(2,1)S(1)} collective-permute-done((bf16[800,128]{1,0:T(8,128)(2,1)S(1)}, bf16[800,128]{1,0:T(8,128)(2,1)S(1)}, u32[]{:S(2)}, u32[]{:S(2)}) %collective-permute-start.28) | collective-permute-done | bytes 204832 | tf_op jit(solution)/shard_map/ppermute | solution.py:452
  104.8 0.9 shard_map.116
  (35 shorter events, 0.1 us)
Async XLA Ops:
  0.6 19.7 %copy-start = (bf16[1,768,768]{2,1,0:T(8,128)(2,1)S(1)}, bf16[1,768,768]{2,1,0:T(8,128)(2,1)}, u32[]{:S(2)}) copy-start(bf16[1,768,768]{2,1,0:T(8,128)(2,1)} %param.12) | copy-start | bytes 3538948
  0.6 22.7 %copy-start.2 = (bf16[1,128,1536]{2,1,0:T(8,128)(2,1)S(1)}, bf16[1,128,1536]{2,1,0:T(8,128)(2,1)}, u32[]{:S(2)}) copy-start(bf16[1,128,1536]{2,1,0:T(8,128)(2,1)} %param.8) | copy-start | bytes 1179652
  0.7 47.8 %copy-start.5 = (s32[1,32,1]{1,2,0:T(1,128)S(1)}, s32[1,32,1]{1,2,0:T(1,128)}, u32[]{:S(2)}) copy-start(s32[1,32,1]{1,2,0:T(1,128)} %param.15) | copy-start | bytes 388
  3.0 5.7 %collective-permute-start = (bf16[96,384]{1,0:T(8,128)(2,1)}, bf16[96,384]{1,0:T(8,128)(2,1)S(1)}, u32[]{:S(2)}, u32[]{:S(2)}) collective-permute-start(bf16[96,384]{1,0:T(8,128)(2,1)} %get-tuple-element.42.refs_0_), channel_id=1, source_target_pairs={{0,8},{8,0},{16,24},{24,16},{1,9},{9,1},{17,25},{25,17},{2,10},{10... | collective-permute-start | bytes 221192 | tf_op jit(solution)/shard_map/ppermute | solution.py:452
  6.1 8.0 %collective-permute-start.1 = (bf16[96,384]{1,0:T(8,128)(2,1)}, bf16[96,384]{1,0:T(8,128)(2,1)S(1)}, u32[]{:S(2)}, u32[]{:S(2)}) collective-permute-start(bf16[96,384]{1,0:T(8,128)(2,1)} %get-tuple-element.42.refs_0_), channel_id=1, source_target_pairs={{0,16},{8,24},{16,0},{24,8},{1,17},{9,25},{17,1},{25,9},{2,18},{10... | collective-permute-start | bytes 221192 | tf_op jit(solution)/shard_map/ppermute | solution.py:452
  8.7 6.5 %collective-permute-start.2 = (bf16[96,384]{1,0:T(8,128)(2,1)}, bf16[96,384]{1,0:T(8,128)(2,1)S(1)}, u32[]{:S(2)}, u32[]{:S(2)}) collective-permute-start(bf16[96,384]{1,0:T(8,128)(2,1)} %get-tuple-element.42.refs_0_), channel_id=1, source_target_pairs={{0,24},{8,16},{16,8},{24,0},{1,25},{9,17},{17,9},{25,1},{2,26},{10... | collective-permute-start | bytes 221192 | tf_op jit(solution)/shard_map/ppermute | solution.py:452
  8.7 9.2 %collective-permute-start.3 = (bf16[96,384]{1,0:T(8,128)(2,1)}, bf16[96,384]{1,0:T(8,128)(2,1)S(1)}, u32[]{:S(2)}, u32[]{:S(2)}) collective-permute-start(bf16[96,384]{1,0:T(8,128)(2,1)} %get-tuple-element.42.refs_0_), channel_id=1, source_target_pairs={{0,1},{1,0},{2,3},{3,2},{4,5},{5,4},{6,7},{7,6},{8,9},{9,8},{10,11... | collective-permute-start | bytes 221192 | tf_op jit(solution)/shard_map/ppermute | solution.py:452
  8.7 9.9 %collective-permute-start.4 = (bf16[96,384]{1,0:T(8,128)(2,1)S(1)}, bf16[96,384]{1,0:T(8,128)(2,1)S(1)}, u32[]{:S(2)}, u32[]{:S(2)}) collective-permute-start(bf16[96,384]{1,0:T(8,128)(2,1)S(1)} %collective-permute-done.refs_1_), channel_id=1, source_target_pairs={{0,1},{1,0},{2,3},{3,2},{4,5},{5,4},{6,7},{7,6},{8,9},{9,8},{10,11... | collective-permute-start | bytes 221192 | tf_op jit(solution)/shard_map/ppermute | solution.py:452
  14.2 4.5 %collective-permute-start.5 = (bf16[96,384]{1,0:T(8,128)(2,1)S(1)}, bf16[96,384]{1,0:T(8,128)(2,1)S(1)}, u32[]{:S(2)}, u32[]{:S(2)}) collective-permute-start(bf16[96,384]{1,0:T(8,128)(2,1)S(1)} %collective-permute-done.1.refs_2_), channel_id=1, source_target_pairs={{0,1},{1,0},{2,3},{3,2},{4,5},{5,4},{6,7},{7,6},{8,9},{9,8},{10,11... | collective-permute-start | bytes 221192 | tf_op jit(solution)/shard_map/ppermute | solution.py:452
  14.2 9.2 %collective-permute-start.10 = (bf16[192,384]{1,0:T(8,128)(2,1)}, bf16[192,384]{1,0:T(8,128)(2,1)S(1)}, u32[]{:S(2)}, u32[]{:S(2)}) collective-permute-start(bf16[192,384]{1,0:T(8,128)(2,1)} %get-tuple-element.44.refs_0_), channel_id=1, source_target_pairs={{0,8},{8,0},{16,24},{24,16},{1,9},{9,1},{17,25},{25,17},{2,10},{10... | collective-permute-start | bytes 442376 | tf_op jit(solution)/shard_map/ppermute | solution.py:452
  15.2 14.2 %collective-permute-start.11 = (bf16[192,384]{1,0:T(8,128)(2,1)}, bf16[192,384]{1,0:T(8,128)(2,1)S(1)}, u32[]{:S(2)}, u32[]{:S(2)}) collective-permute-start(bf16[192,384]{1,0:T(8,128)(2,1)} %get-tuple-element.44.refs_0_), channel_id=1, source_target_pairs={{0,16},{8,24},{16,0},{24,8},{1,17},{9,25},{17,1},{25,9},{2,18},{10... | collective-permute-start | bytes 442376 | tf_op jit(solution)/shard_map/ppermute | solution.py:452
  18.0 12.9 %collective-permute-start.12 = (bf16[192,384]{1,0:T(8,128)(2,1)}, bf16[192,384]{1,0:T(8,128)(2,1)S(1)}, u32[]{:S(2)}, u32[]{:S(2)}) collective-permute-start(bf16[192,384]{1,0:T(8,128)(2,1)} %get-tuple-element.44.refs_0_), channel_id=1, source_target_pairs={{0,24},{8,16},{16,8},{24,0},{1,25},{9,17},{17,9},{25,1},{2,26},{10... | collective-permute-start | bytes 442376 | tf_op jit(solution)/shard_map/ppermute | solution.py:452
  18.7 13.7 %collective-permute-start.13 = (bf16[192,384]{1,0:T(8,128)(2,1)}, bf16[192,384]{1,0:T(8,128)(2,1)S(1)}, u32[]{:S(2)}, u32[]{:S(2)}) collective-permute-start(bf16[192,384]{1,0:T(8,128)(2,1)} %get-tuple-element.44.refs_0_), channel_id=1, source_target_pairs={{0,1},{1,0},{2,3},{3,2},{4,5},{5,4},{6,7},{7,6},{8,9},{9,8},{10,11... | collective-permute-start | bytes 442376 | tf_op jit(solution)/shard_map/ppermute | solution.py:452
  18.7 1.7 %collective-permute-start.6 = (bf16[96,384]{1,0:T(8,128)(2,1)S(1)}, bf16[96,384]{1,0:T(8,128)(2,1)S(1)}, u32[]{:S(2)}, u32[]{:S(2)}) collective-permute-start(bf16[96,384]{1,0:T(8,128)(2,1)S(1)} %collective-permute-done.2.refs_3_), channel_id=1, source_target_pairs={{0,1},{1,0},{2,3},{3,2},{4,5},{5,4},{6,7},{7,6},{8,9},{9,8},{10,11... | collective-permute-start | bytes 221192 | tf_op jit(solution)/shard_map/ppermute | solution.py:452
  20.4 61.2 %collective-permute-start.22 = (bf16[768,768]{1,0:T(8,128)(2,1)S(1)}, bf16[768,768]{1,0:T(8,128)(2,1)S(1)}, u32[]{:S(2)}, u32[]{:S(2)}) collective-permute-start(bf16[768,768]{1,0:T(8,128)(2,1)S(1)} %bitcast.12), channel_id=1, source_target_pairs={{0,1},{1,0},{2,3},{3,2},{4,5},{5,4},{6,7},{7,6},{8,9},{9,8},{10,11... | collective-permute-start | bytes 3538952 | tf_op jit(solution)/shard_map/ppermute | solution.py:452
  23.4 58.2 %collective-permute-start.23 = (bf16[768,768]{1,0:T(8,128)(2,1)}, bf16[768,768]{1,0:T(8,128)(2,1)S(1)}, u32[]{:S(2)}, u32[]{:S(2)}) collective-permute-start(bf16[768,768]{1,0:T(8,128)(2,1)} %bitcast.14), channel_id=1, source_target_pairs={{0,1},{1,0},{2,3},{3,2},{4,5},{5,4},{6,7},{7,6},{8,9},{9,8},{10,11... | collective-permute-start | bytes 3538952 | tf_op jit(solution)/shard_map/ppermute | solution.py:452
  29.4 11.3 %collective-permute-start.7 = (bf16[128,1536]{1,0:T(8,128)(2,1)S(1)}, bf16[128,1536]{1,0:T(8,128)(2,1)S(1)}, u32[]{:S(2)}, u32[]{:S(2)}) collective-permute-start(bf16[128,1536]{1,0:T(8,128)(2,1)S(1)} %shard_map.106.refs_0_), channel_id=1, source_target_pairs={{0,2},{1,3},{2,0},{3,1},{4,6},{5,7},{6,4},{7,5},{8,10},{9,11},{10,... | collective-permute-start | bytes 1179656 | tf_op jit(solution)/shard_map/ppermute | solution.py:452
  30.9 17.0 %collective-permute-start.8 = (bf16[128,1536]{1,0:T(8,128)(2,1)S(1)}, bf16[128,1536]{1,0:T(8,128)(2,1)S(1)}, u32[]{:S(2)}, u32[]{:S(2)}) collective-permute-start(bf16[128,1536]{1,0:T(8,128)(2,1)S(1)} %shard_map.106.refs_0_), channel_id=1, source_target_pairs={{0,4},{1,5},{2,6},{3,7},{4,0},{5,1},{6,2},{7,3},{8,12},{9,13},{10,... | collective-permute-start | bytes 1179656 | tf_op jit(solution)/shard_map/ppermute | solution.py:452
  32.4 15.5 %collective-permute-start.9 = (bf16[128,1536]{1,0:T(8,128)(2,1)S(1)}, bf16[128,1536]{1,0:T(8,128)(2,1)S(1)}, u32[]{:S(2)}, u32[]{:S(2)}) collective-permute-start(bf16[128,1536]{1,0:T(8,128)(2,1)S(1)} %shard_map.106.refs_0_), channel_id=1, source_target_pairs={{0,6},{1,7},{2,4},{3,5},{4,2},{5,3},{6,0},{7,1},{8,14},{9,15},{10,... | collective-permute-start | bytes 1179656 | tf_op jit(solution)/shard_map/ppermute | solution.py:452
  40.6 9.8 %collective-permute-start.14 = (bf16[192,384]{1,0:T(8,128)(2,1)S(1)}, bf16[192,384]{1,0:T(8,128)(2,1)S(1)}, u32[]{:S(2)}, u32[]{:S(2)}) collective-permute-start(bf16[192,384]{1,0:T(8,128)(2,1)S(1)} %collective-permute-done.10.refs_1_), channel_id=1, source_target_pairs={{0,1},{1,0},{2,3},{3,2},{4,5},{5,4},{6,7},{7,6},{8,9},{9,8},{10,11... | collective-permute-start | bytes 442376 | tf_op jit(solution)/shard_map/ppermute | solution.py:452
  47.9 4.2 %collective-permute-start.15 = (bf16[192,384]{1,0:T(8,128)(2,1)S(1)}, bf16[192,384]{1,0:T(8,128)(2,1)S(1)}, u32[]{:S(2)}, u32[]{:S(2)}) collective-permute-start(bf16[192,384]{1,0:T(8,128)(2,1)S(1)} %collective-permute-done.11.refs_2_), channel_id=1, source_target_pairs={{0,1},{1,0},{2,3},{3,2},{4,5},{5,4},{6,7},{7,6},{8,9},{9,8},{10,11... | collective-permute-start | bytes 442376 | tf_op jit(solution)/shard_map/ppermute | solution.py:452
  47.9 5.7 %collective-permute-start.16 = (bf16[192,384]{1,0:T(8,128)(2,1)S(1)}, bf16[192,384]{1,0:T(8,128)(2,1)S(1)}, u32[]{:S(2)}, u32[]{:S(2)}) collective-permute-start(bf16[192,384]{1,0:T(8,128)(2,1)S(1)} %collective-permute-done.12.refs_3_), channel_id=1, source_target_pairs={{0,1},{1,0},{2,3},{3,2},{4,5},{5,4},{6,7},{7,6},{8,9},{9,8},{10,11... | collective-permute-start | bytes 442376 | tf_op jit(solution)/shard_map/ppermute | solution.py:452
  48.6 0.9 copy-start.4
  49.7 4.4 %copy-start.3 = (bf16[192,384]{1,0:T(8,128)(2,1)S(1)}, bf16[192,384]{1,0:T(8,128)(2,1)}, u32[]{:S(2)}) copy-start(bf16[192,384]{1,0:T(8,128)(2,1)} %get-tuple-element.44.refs_0_) | copy-start | bytes 442372
  50.5 8.2 %collective-permute-start.24 = (bf16[208,512]{1,0:T(8,128)(2,1)S(1)}, bf16[208,512]{1,0:T(8,128)(2,1)S(1)}, u32[]{:S(2)}, u32[]{:S(2)}) collective-permute-start(bf16[208,512]{1,0:T(8,128)(2,1)S(1)} %get-tuple-element.49.refs_0_), channel_id=1, source_target_pairs={{0,2},{1,3},{2,0},{3,1},{4,6},{5,7},{6,4},{7,5},{8,10},{9,11},{10,... | collective-permute-start | bytes 638984 | tf_op jit(solution)/shard_map/ppermute | solution.py:452
  52.0 10.7 %collective-permute-start.25 = (bf16[208,512]{1,0:T(8,128)(2,1)S(1)}, bf16[208,512]{1,0:T(8,128)(2,1)S(1)}, u32[]{:S(2)}, u32[]{:S(2)}) collective-permute-start(bf16[208,512]{1,0:T(8,128)(2,1)S(1)} %get-tuple-element.49.refs_0_), channel_id=1, source_target_pairs={{0,4},{1,5},{2,6},{3,7},{4,0},{5,1},{6,2},{7,3},{8,12},{9,13},{10,... | collective-permute-start | bytes 638984 | tf_op jit(solution)/shard_map/ppermute | solution.py:452
  53.6 10.7 %collective-permute-start.26 = (bf16[208,512]{1,0:T(8,128)(2,1)S(1)}, bf16[208,512]{1,0:T(8,128)(2,1)S(1)}, u32[]{:S(2)}, u32[]{:S(2)}) collective-permute-start(bf16[208,512]{1,0:T(8,128)(2,1)S(1)} %get-tuple-element.49.refs_0_), channel_id=1, source_target_pairs={{0,6},{1,7},{2,4},{3,5},{4,2},{5,3},{6,0},{7,1},{8,14},{9,15},{10,... | collective-permute-start | bytes 638984 | tf_op jit(solution)/shard_map/ppermute | solution.py:452
  58.7 8.7 %collective-permute-start.17 = (bf16[2,192,128]{2,1,0:T(8,128)(2,1)S(1)}, bf16[2,192,128]{2,1,0:T(8,128)(2,1)S(1)}, u32[]{:S(2)}, u32[]{:S(2)}) collective-permute-start(bf16[2,192,128]{2,1,0:T(8,128)(2,1)S(1)} %get-tuple-element.46), channel_id=1, source_target_pairs={{0,2},{1,3},{2,0},{3,1},{4,6},{5,7},{6,4},{7,5},{8,10},{9,11},{10,... | collective-permute-start | bytes 294920 | tf_op jit(solution)/shard_map/ppermute | solution.py:452
  64.7 17.0 %copy-start.1 = (bf16[1,768,768]{2,1,0:T(8,128)(2,1)S(1)}, bf16[1,768,768]{2,1,0:T(8,128)(2,1)}, u32[]{:S(2)}) copy-start(bf16[1,768,768]{2,1,0:T(8,128)(2,1)} %param.13) | copy-start | bytes 3538948
  65.3 9.6 %collective-permute-start.30 = (bf16[2,192,256]{2,1,0:T(8,128)(2,1)S(1)}, bf16[2,192,256]{2,1,0:T(8,128)(2,1)S(1)}, u32[]{:S(2)}, u32[]{:S(2)}) collective-permute-start(bf16[2,192,256]{2,1,0:T(8,128)(2,1)S(1)} %get-tuple-element.74), channel_id=1, source_target_pairs={{0,2},{1,3},{2,0},{3,1},{4,6},{5,7},{6,4},{7,5},{8,10},{9,11},{10,... | collective-permute-start | bytes 589832 | tf_op jit(solution)/shard_map/ppermute | solution.py:452
  66.8 6.3 %collective-permute-start.18 = (bf16[2,192,128]{2,1,0:T(8,128)(2,1)S(1)}, bf16[2,192,128]{2,1,0:T(8,128)(2,1)S(1)}, u32[]{:S(2)}, u32[]{:S(2)}) collective-permute-start(bf16[2,192,128]{2,1,0:T(8,128)(2,1)S(1)} %get-tuple-element.47), channel_id=1, source_target_pairs={{0,4},{1,5},{2,6},{3,7},{4,0},{5,1},{6,2},{7,3},{8,12},{9,13},{10,... | collective-permute-start | bytes 294920 | tf_op jit(solution)/shard_map/ppermute | solution.py:452
  67.4 5.8 %collective-permute-start.19 = (bf16[2,192,128]{2,1,0:T(8,128)(2,1)S(1)}, bf16[2,192,128]{2,1,0:T(8,128)(2,1)S(1)}, u32[]{:S(2)}, u32[]{:S(2)}) collective-permute-start(bf16[2,192,128]{2,1,0:T(8,128)(2,1)S(1)} %get-tuple-element.48), channel_id=1, source_target_pairs={{0,6},{1,7},{2,4},{3,5},{4,2},{5,3},{6,0},{7,1},{8,14},{9,15},{10,... | collective-permute-start | bytes 294920 | tf_op jit(solution)/shard_map/ppermute | solution.py:452
  73.1 7.8 %collective-permute-start.31 = (bf16[2,192,256]{2,1,0:T(8,128)(2,1)S(1)}, bf16[2,192,256]{2,1,0:T(8,128)(2,1)S(1)}, u32[]{:S(2)}, u32[]{:S(2)}) collective-permute-start(bf16[2,192,256]{2,1,0:T(8,128)(2,1)S(1)} %get-tuple-element.75), channel_id=1, source_target_pairs={{0,4},{1,5},{2,6},{3,7},{4,0},{5,1},{6,2},{7,3},{8,12},{9,13},{10,... | collective-permute-start | bytes 589832 | tf_op jit(solution)/shard_map/ppermute | solution.py:452
  73.2 7.7 %collective-permute-start.32 = (bf16[2,192,256]{2,1,0:T(8,128)(2,1)S(1)}, bf16[2,192,256]{2,1,0:T(8,128)(2,1)S(1)}, u32[]{:S(2)}, u32[]{:S(2)}) collective-permute-start(bf16[2,192,256]{2,1,0:T(8,128)(2,1)S(1)} %get-tuple-element.76), channel_id=1, source_target_pairs={{0,6},{1,7},{2,4},{3,5},{4,2},{5,3},{6,0},{7,1},{8,14},{9,15},{10,... | collective-permute-start | bytes 589832 | tf_op jit(solution)/shard_map/ppermute | solution.py:452
  74.9 16.6 %collective-permute-start.20 = (bf16[2,768,128]{2,1,0:T(8,128)(2,1)S(1)}, bf16[2,768,128]{2,1,0:T(8,128)(2,1)S(1)}, u32[]{:S(2)}, u32[]{:S(2)}) collective-permute-start(bf16[2,768,128]{2,1,0:T(8,128)(2,1)S(1)} %shard_map.110.refs_0_), channel_id=1, source_target_pairs={{0,1},{1,0},{2,3},{3,2},{4,5},{5,4},{6,7},{7,6},{8,9},{9,8},{10,11... | collective-permute-start | bytes 1179656 | tf_op jit(solution)/shard_map/ppermute | solution.py:452
  80.9 2.5 %collective-permute-start.21 = (s32[1,1]{1,0:T(1,128)}, s32[1,1]{1,0:T(1,128)}, u32[]{:S(2)}, u32[]{:S(2)}) collective-permute-start(s32[1,1]{1,0:T(1,128)} %param.14), channel_id=1, source_target_pairs={{0,1},{1,0},{2,3},{3,2},{4,5},{5,4},{6,7},{7,6},{8,9},{9,8},{10,11... | collective-permute-start | bytes 20 | tf_op jit(solution)/shard_map/ppermute | solution.py:452
  81.0 15.9 %collective-permute-start.33 = (bf16[2,768,128]{2,1,0:T(8,128)(2,1)S(1)}, bf16[2,768,128]{2,1,0:T(8,128)(2,1)S(1)}, u32[]{:S(2)}, u32[]{:S(2)}) collective-permute-start(bf16[2,768,128]{2,1,0:T(8,128)(2,1)S(1)} %get-tuple-element.78), channel_id=1, source_target_pairs={{0,1},{1,0},{2,3},{3,2},{4,5},{5,4},{6,7},{7,6},{8,9},{9,8},{10,11... | collective-permute-start | bytes 1179656 | tf_op jit(solution)/shard_map/ppermute | solution.py:452
  93.3 8.0 %collective-permute-start.27 = (bf16[800,128]{1,0:T(8,128)(2,1)S(1)}, bf16[800,128]{1,0:T(8,128)(2,1)S(1)}, u32[]{:S(2)}, u32[]{:S(2)}) collective-permute-start(bf16[800,128]{1,0:T(8,128)(2,1)S(1)} %get-tuple-element.65), channel_id=1, source_target_pairs={{0,2},{1,3},{2,0},{3,1},{4,6},{5,7},{6,4},{7,5},{8,10},{9,11},{10,... | collective-permute-start | bytes 614408 | tf_op jit(solution)/shard_map/ppermute | solution.py:452
  93.4 11.4 %collective-permute-start.28 = (bf16[800,128]{1,0:T(8,128)(2,1)S(1)}, bf16[800,128]{1,0:T(8,128)(2,1)S(1)}, u32[]{:S(2)}, u32[]{:S(2)}) collective-permute-start(bf16[800,128]{1,0:T(8,128)(2,1)S(1)} %get-tuple-element.66), channel_id=1, source_target_pairs={{0,4},{1,5},{2,6},{3,7},{4,0},{5,1},{6,2},{7,3},{8,12},{9,13},{10,... | collective-permute-start | bytes 614408 | tf_op jit(solution)/shard_map/ppermute | solution.py:452
  95.2 9.6 %collective-permute-start.29 = (bf16[800,128]{1,0:T(8,128)(2,1)S(1)}, bf16[800,128]{1,0:T(8,128)(2,1)S(1)}, u32[]{:S(2)}, u32[]{:S(2)}) collective-permute-start(bf16[800,128]{1,0:T(8,128)(2,1)S(1)} %get-tuple-element.67), channel_id=1, source_target_pairs={{0,6},{1,7},{2,4},{3,5},{4,2},{5,3},{6,0},{7,1},{8,14},{9,15},{10,... | collective-permute-start | bytes 614408 | tf_op jit(solution)/shard_map/ppermute | solution.py:452
